TPU v7x, 256 devices: a whole 4x4x8 slice. The times are simulated.
256 devices in a mesh: gx: 8 (over y, core), gy: 32 (over x, z).
Axes of the slice: x: 4, y: 4, z: 8, core: 2. Of those that a mesh axis runs over, the one named last changes fastest.
Arguments:
- source: float32 [64, 32, 4096], P(None, 'gx', 'gy'), may hold values from -6 to 6
- initial: float32 [64, 32, 4096], P(None, 'gx', 'gy'), may hold values from -6 to 6
- reaction: float32 [64, 32, 4096], P(None, 'gx', 'gy'), may hold values from 1 to 3
- stiffness: float32 [32, 4096], P('gx', 'gy'), may hold values from 0.5 to 2
- line_op: float32 [8, 8], replicated, may hold values from -1.6 to 5.6
- face_deriv: float32 [8], replicated, may hold values from -2 to 2
- wall_flags: int32 [4, 32, 4096], P(None, 'gx', 'gy'), may hold values 0 or 1
Outputs:
- hessenberg: float32 [6, 5], replicated
- krylov_basis: float32 [6, 64, 32, 4096], P(None, None, 'gx', 'gy')
All inputs are finite; a program needn't handle non-finite values. No bound on the sum of `wall_flags` on one device may be relied on, other than what follows from the above.
Results may differ from a plain program's by a relative error of at most 0.0003.
Values sent between devices are 32-bit elements; how exact they have to be, the bound alone decides.
A program may use at most 64 MiB of HBM per device.

v0:
```python
import jax
import jax.numpy as jnp
from jax import lax
from jax.sharding import Mesh
from jax.sharding import PartitionSpec as P

P_SIZE = 8
ITERS = 5
GX = ("gx_0", "gx_1")
GY = ("gy_0", "gy_1")


TAU = 2.0
FLOOR = 0.1


def extended(array, sides, width):
    for axis, dim in sides:
        devices, length = (lax.axis_size(axis), array.shape[dim])
        up = [(i, (i + 1) % devices) for i in range(devices)]
        down = [(j, i) for i, j in up]
        last = lax.slice_in_dim(array, length - width, length, axis=dim)
        leading = lax.slice_in_dim(array, 0, width, axis=dim)
        before = lax.ppermute(last, axis, up)
        after = lax.ppermute(leading, axis, down)
        array = jnp.concatenate([before, array, after], axis=dim)
    return array


def sent_to_all(array, axis):
    copies = jnp.broadcast_to(array, (lax.axis_size(axis), *array.shape))
    return lax.all_to_all(copies, axis, split_axis=0, concat_axis=0, tiled=True)


def over_copies(array, axis):
    everything = sent_to_all(array, axis)
    return jnp.sum(everything, axis=0)


def by_axis(array, axes):
    far, near = axes
    nearer = over_copies(array, near)
    return over_copies(nearer, far)


def together(arrays, axis):
    vector, at, gathered = (jnp.concatenate([a.reshape(-1) for a in arrays]), 0, [])
    subtotal = by_axis(vector, axis)
    for a in arrays:
        gathered.append(subtotal[at : at + a.size].reshape(a.shape))
        at += a.size
    return tuple(gathered)


def local_total(values):
    return jnp.sum(jnp.sum(values, axis=0))


def x_traces(nodes, face_deriv):
    highest = lax.Precision.HIGHEST
    lower = jnp.einsum("c,cbxy->bxy", face_deriv, nodes, precision=highest)
    upper = jnp.einsum("c,cbxy->bxy", face_deriv[::-1], nodes, precision=highest)
    return jnp.stack([nodes[0], lower, nodes[-1], upper])


def y_traces(nodes, face_deriv):
    highest = lax.Precision.HIGHEST
    lower = jnp.einsum("c,acxy->axy", face_deriv, nodes, precision=highest)
    upper = jnp.einsum("c,acxy->axy", face_deriv[::-1], nodes, precision=highest)
    return jnp.stack([nodes[:, 0], lower, nodes[:, -1], upper])


def apply_op(field, reaction, stiffness, line_op, face_deriv, opened):
    highest = lax.Precision.HIGHEST
    nodes = field.reshape(P_SIZE, P_SIZE, field.shape[1], field.shape[2])
    interior = stiffness * (
        jnp.einsum("ac,cbxy->abxy", line_op, nodes, precision=highest)
        + jnp.einsum("bc,acxy->abxy", line_op, nodes, precision=highest)
    )
    xside = extended(x_traces(nodes, face_deriv), ((GX, 2),), 1)
    yside = extended(y_traces(nodes, face_deriv), ((GY, 3),), 1)
    x_own = xside[:, :, 1:-1]
    y_own = yside[:, :, :, 1:-1]
    east_nb = xside[0:2, :, 2:]
    west_nb = xside[2:4, :, :-2]
    north_nb = yside[0:2, :, :, 2:]
    south_nb = yside[2:4, :, :, :-2]
    add_east = TAU * (x_own[2] - opened[1] * east_nb[0]) + 0.5 * (x_own[3] - opened[1] * east_nb[1])
    add_west = TAU * (x_own[0] - opened[0] * west_nb[0]) + 0.5 * (x_own[1] - opened[0] * west_nb[1])
    add_north = TAU * (y_own[2] - opened[3] * north_nb[0]) + 0.5 * (
        y_own[3] - opened[3] * north_nb[1]
    )
    add_south = TAU * (y_own[0] - opened[2] * south_nb[0]) + 0.5 * (
        y_own[1] - opened[2] * south_nb[1]
    )
    result = reaction.reshape(nodes.shape) * nodes + interior
    result = result.at[0].add(add_west).at[P_SIZE - 1].add(add_east)
    result = result.at[:, 0].add(add_south).at[:, P_SIZE - 1].add(add_north)
    return result.reshape(field.shape)


def norm_scale(vector, total):
    squares = by_axis(local_total(vector * vector), (("gx_0", "gx_1"), ("gy_0", "gy_1")))
    return jnp.sqrt(squares / total + FLOOR)


def body(source, initial, reaction, stiffness, line_op, face_deriv, wall_flags):
    highest = lax.Precision.HIGHEST
    total = float(
        P_SIZE * P_SIZE * source.shape[1] * lax.axis_size(GX) * source.shape[2] * lax.axis_size(GY)
    )
    opened = 1.0 - wall_flags.astype(jnp.float32)

    def operate(field):
        return apply_op(field, reaction, stiffness, line_op, face_deriv, opened)

    def products(basis, image):
        per_cell = jnp.einsum("kqxy,qxy->kxy", basis, image, precision=highest)
        return jnp.sum(per_cell, axis=(1, 2))

    first = source - operate(initial)
    basis = jnp.zeros((ITERS + 1,) + source.shape, jnp.float32)
    hessen = jnp.zeros((ITERS + 1, ITERS), jnp.float32)
    rows = lax.broadcasted_iota(jnp.int32, (ITERS + 1, ITERS), 0)
    cols = lax.broadcasted_iota(jnp.int32, (ITERS + 1, ITERS), 1)
    slots = lax.broadcasted_iota(jnp.int32, (ITERS + 1,), 0)

    def advance(step, carry):
        basis, hessen, pending = carry
        image = operate(pending)
        local = products(basis, image)
        projected, crossed, squares = together(
            (local, local_total(pending * image), local_total(pending * pending)),
            (("gx_0", "gx_1"), ("gy_0", "gy_1")),
        )
        beta = jnp.sqrt(squares / total + FLOOR)
        basis = lax.dynamic_update_index_in_dim(basis, pending / beta, step, 0)
        coeffs = projected / (total * beta) + jnp.where(
            slots == step, crossed / (total * beta * beta), 0.0
        )
        pending = image / beta - jnp.einsum("k,kqxy->qxy", coeffs, basis, precision=highest)
        hessen = hessen + jnp.where(cols == step, coeffs[:, None], 0.0)
        hessen = hessen + jnp.where((rows == step) & (cols == step - 1), beta, 0.0)
        return (basis, hessen, pending)

    basis, hessen, pending = lax.fori_loop(0, ITERS, advance, (basis, hessen, first))
    beta = norm_scale(pending, total)
    basis = basis.at[ITERS].set(pending / beta)
    hessen = hessen + jnp.where((rows == ITERS) & (cols == ITERS - 1), beta, 0.0)
    return (hessen, basis)


def solution(mesh):
    finer = Mesh(mesh.devices.reshape(4, 2, 4, 8), ("gx_0", "gx_1", "gy_0", "gy_1"))
    placed = (
        P(None, GX, GY),
        P(None, GX, GY),
        P(None, GX, GY),
        P(GX, GY),
        P(),
        P(),
        P(None, GX, GY),
    )
    return jax.shard_map(
        body, mesh=finer, in_specs=placed, out_specs=(P(), P(None, None, GX, GY)), check_vma=False
    )
```

profile of v0, /device:TPU:1, one launch (start us, length us, event | category | flops | bytes accessed | tf_op | source)
XLA Modules:
  0.0 283.4 jit_solution(14238751675292075828)
XLA Ops:
  2.2 2.7 collective-permute-start.4
  7.3 6.2 %collective-permute-start.7 = (f32[4,8,4,1]{3,1,2,0:T(8,128)S(1)}, f32[4,8,4,1]{3,1,2,0:T(8,128)S(1)}, u32[]{:S(2)}, u32[]{:S(2)}) collective-permute-start(f32[4,8,4,1]{3,1,2,0:T(8,128)S(1)} %get-tuple-element.670), channel_id=1, source_target_pairs={{1,0},{2,1},{3,2},{4,3},{5,4},{6,5},{7,6},{8,7},{9,8},{10,9},{11,1... | collective-permute-start | bytes 1544 | tf_op jit(solution)/shard_map/ppermute | solution.py:25
  17.0 239.6 %while.31 = (s32[]{:T(128)}, f32[6,64,4,128]{3,1,2,0:T(8,128)S(1)}, f32[6,5]{1,0:T(8,128)S(1)}, f32[64,4,128]{2,0,1:T(8,128)S(1)}, f32[64,4,128]{2,0,1:T(8,128)S...) while((s32[]{:T(128)}, f32[6,64,4,128]{3,1,2,0:T(8,128)S(1)}, ...), condition=%wide.region_5.6_spmd.clone.clone, body=%wide.region_0.5_spmd.clone.clone.sunk | while | flops 13279853 | bytes 6174235 | solution.py:146
  21.0 4.8 %collective-permute-start.3 = (f32[4,8,4,1]{3,1,2,0:T(8,128)S(1)}, f32[4,8,4,1]{3,1,2,0:T(8,128)S(1)}, u32[]{:S(2)}, u32[]{:S(2)}) collective-permute-start(f32[4,8,4,1]{3,1,2,0:T(8,128)S(1)} %get-tuple-element.765), channel_id=1, source_target_pairs={{1,0},{2,1},{3,2},{4,3},{5,4},{6,5},{7,6},{8,7},{9,8},{10,9},{11,1... | collective-permute-start | bytes 1544 | tf_op jit(solution)/shard_map/while/body/eval_jaxpr/ppermute | solution.py:25
  28.3 2.6 convolution_bitcast_fusion.2
  33.0 6.4 %all-to-all-start = ((f32[32,1,8]{2,1,0:T(1,128)}), f32[32,1,8]{2,1,0:T(1,128)S(1)}, u32[]{:S(2)}, u32[]{:S(2)}) async-start(f32[32,1,8]{2,1,0:T(1,128)} %broadcast_in_dim.147), calls=%async_computation | async-start | bytes 32768 | tf_op jit(solution)/shard_map/while/body/eval_jaxpr/all_to_all | solution.py:32
  39.4 8.6 %all-to-all-done = f32[32,1,8]{2,1,0:T(1,128)S(1)} async-done(((f32[32,1,8]{2,1,0:T(1,128)}), f32[32,1,8]{2,1,0:T(1,128)S(1)}, u32[]{:S(2)}, u32[]{:S(2)}) %all-to-all-start) | async-done | bytes 1056 | tf_op jit(solution)/shard_map/while/body/eval_jaxpr/all_to_all | solution.py:32
  48.6 9.0 %all-to-all-start.1 = ((f32[8,1,8]{2,1,0:T(1,128)}), f32[8,1,8]{2,1,0:T(1,128)S(1)}, u32[]{:S(2)}, u32[]{:S(2)}) async-start(f32[8,1,8]{2,1,0:T(1,128)} %broadcast_in_dim.148), calls=%async_computation.1 | async-start | bytes 8192 | tf_op jit(solution)/shard_map/while/body/eval_jaxpr/all_to_all | solution.py:32
  57.6 4.5 %all-to-all-done.1 = f32[8,1,8]{2,1,0:T(1,128)S(1)} async-done(((f32[8,1,8]{2,1,0:T(1,128)}), f32[8,1,8]{2,1,0:T(1,128)S(1)}, u32[]{:S(2)}, u32[]{:S(2)}) %all-to-all-start.1) | async-done | bytes 288 | tf_op jit(solution)/shard_map/while/body/eval_jaxpr/all_to_all | solution.py:32
  69.0 4.5 %collective-permute-start.3 = (f32[4,8,4,1]{3,1,2,0:T(8,128)S(1)}, f32[4,8,4,1]{3,1,2,0:T(8,128)S(1)}, u32[]{:S(2)}, u32[]{:S(2)}) collective-permute-start(f32[4,8,4,1]{3,1,2,0:T(8,128)S(1)} %get-tuple-element.765), channel_id=1, source_target_pairs={{1,0},{2,1},{3,2},{4,3},{5,4},{6,5},{7,6},{8,7},{9,8},{10,9},{11,1... | collective-permute-start | bytes 1544 | tf_op jit(solution)/shard_map/while/body/eval_jaxpr/ppermute | solution.py:25
  80.7 6.4 %all-to-all-start = ((f32[32,1,8]{2,1,0:T(1,128)}), f32[32,1,8]{2,1,0:T(1,128)S(1)}, u32[]{:S(2)}, u32[]{:S(2)}) async-start(f32[32,1,8]{2,1,0:T(1,128)} %broadcast_in_dim.147), calls=%async_computation | async-start | bytes 32768 | tf_op jit(solution)/shard_map/while/body/eval_jaxpr/all_to_all | solution.py:32
  87.1 8.6 %all-to-all-done = f32[32,1,8]{2,1,0:T(1,128)S(1)} async-done(((f32[32,1,8]{2,1,0:T(1,128)}), f32[32,1,8]{2,1,0:T(1,128)S(1)}, u32[]{:S(2)}, u32[]{:S(2)}) %all-to-all-start) | async-done | bytes 1056 | tf_op jit(solution)/shard_map/while/body/eval_jaxpr/all_to_all | solution.py:32
  96.3 8.8 %all-to-all-start.1 = ((f32[8,1,8]{2,1,0:T(1,128)}), f32[8,1,8]{2,1,0:T(1,128)S(1)}, u32[]{:S(2)}, u32[]{:S(2)}) async-start(f32[8,1,8]{2,1,0:T(1,128)} %broadcast_in_dim.148), calls=%async_computation.1 | async-start | bytes 8192 | tf_op jit(solution)/shard_map/while/body/eval_jaxpr/all_to_all | solution.py:32
  105.2 4.5 %all-to-all-done.1 = f32[8,1,8]{2,1,0:T(1,128)S(1)} async-done(((f32[8,1,8]{2,1,0:T(1,128)}), f32[8,1,8]{2,1,0:T(1,128)S(1)}, u32[]{:S(2)}, u32[]{:S(2)}) %all-to-all-start.1) | async-done | bytes 288 | tf_op jit(solution)/shard_map/while/body/eval_jaxpr/all_to_all | solution.py:32
  116.6 4.5 %collective-permute-start.3 = (f32[4,8,4,1]{3,1,2,0:T(8,128)S(1)}, f32[4,8,4,1]{3,1,2,0:T(8,128)S(1)}, u32[]{:S(2)}, u32[]{:S(2)}) collective-permute-start(f32[4,8,4,1]{3,1,2,0:T(8,128)S(1)} %get-tuple-element.765), channel_id=1, source_target_pairs={{1,0},{2,1},{3,2},{4,3},{5,4},{6,5},{7,6},{8,7},{9,8},{10,9},{11,1... | collective-permute-start | bytes 1544 | tf_op jit(solution)/shard_map/while/body/eval_jaxpr/ppermute | solution.py:25
  128.3 6.4 %all-to-all-start = ((f32[32,1,8]{2,1,0:T(1,128)}), f32[32,1,8]{2,1,0:T(1,128)S(1)}, u32[]{:S(2)}, u32[]{:S(2)}) async-start(f32[32,1,8]{2,1,0:T(1,128)} %broadcast_in_dim.147), calls=%async_computation | async-start | bytes 32768 | tf_op jit(solution)/shard_map/while/body/eval_jaxpr/all_to_all | solution.py:32
  134.7 8.6 %all-to-all-done = f32[32,1,8]{2,1,0:T(1,128)S(1)} async-done(((f32[32,1,8]{2,1,0:T(1,128)}), f32[32,1,8]{2,1,0:T(1,128)S(1)}, u32[]{:S(2)}, u32[]{:S(2)}) %all-to-all-start) | async-done | bytes 1056 | tf_op jit(solution)/shard_map/while/body/eval_jaxpr/all_to_all | solution.py:32
  143.9 8.8 %all-to-all-start.1 = ((f32[8,1,8]{2,1,0:T(1,128)}), f32[8,1,8]{2,1,0:T(1,128)S(1)}, u32[]{:S(2)}, u32[]{:S(2)}) async-start(f32[8,1,8]{2,1,0:T(1,128)} %broadcast_in_dim.148), calls=%async_computation.1 | async-start | bytes 8192 | tf_op jit(solution)/shard_map/while/body/eval_jaxpr/all_to_all | solution.py:32
  152.7 4.5 %all-to-all-done.1 = f32[8,1,8]{2,1,0:T(1,128)S(1)} async-done(((f32[8,1,8]{2,1,0:T(1,128)}), f32[8,1,8]{2,1,0:T(1,128)S(1)}, u32[]{:S(2)}, u32[]{:S(2)}) %all-to-all-start.1) | async-done | bytes 288 | tf_op jit(solution)/shard_map/while/body/eval_jaxpr/all_to_all | solution.py:32
  164.2 4.5 %collective-permute-start.3 = (f32[4,8,4,1]{3,1,2,0:T(8,128)S(1)}, f32[4,8,4,1]{3,1,2,0:T(8,128)S(1)}, u32[]{:S(2)}, u32[]{:S(2)}) collective-permute-start(f32[4,8,4,1]{3,1,2,0:T(8,128)S(1)} %get-tuple-element.765), channel_id=1, source_target_pairs={{1,0},{2,1},{3,2},{4,3},{5,4},{6,5},{7,6},{8,7},{9,8},{10,9},{11,1... | collective-permute-start | bytes 1544 | tf_op jit(solution)/shard_map/while/body/eval_jaxpr/ppermute | solution.py:25
  175.9 6.4 %all-to-all-start = ((f32[32,1,8]{2,1,0:T(1,128)}), f32[32,1,8]{2,1,0:T(1,128)S(1)}, u32[]{:S(2)}, u32[]{:S(2)}) async-start(f32[32,1,8]{2,1,0:T(1,128)} %broadcast_in_dim.147), calls=%async_computation | async-start | bytes 32768 | tf_op jit(solution)/shard_map/while/body/eval_jaxpr/all_to_all | solution.py:32
  182.2 8.6 %all-to-all-done = f32[32,1,8]{2,1,0:T(1,128)S(1)} async-done(((f32[32,1,8]{2,1,0:T(1,128)}), f32[32,1,8]{2,1,0:T(1,128)S(1)}, u32[]{:S(2)}, u32[]{:S(2)}) %all-to-all-start) | async-done | bytes 1056 | tf_op jit(solution)/shard_map/while/body/eval_jaxpr/all_to_all | solution.py:32
  191.5 8.8 %all-to-all-start.1 = ((f32[8,1,8]{2,1,0:T(1,128)}), f32[8,1,8]{2,1,0:T(1,128)S(1)}, u32[]{:S(2)}, u32[]{:S(2)}) async-start(f32[8,1,8]{2,1,0:T(1,128)} %broadcast_in_dim.148), calls=%async_computation.1 | async-start | bytes 8192 | tf_op jit(solution)/shard_map/while/body/eval_jaxpr/all_to_all | solution.py:32
  200.3 4.5 %all-to-all-done.1 = f32[8,1,8]{2,1,0:T(1,128)S(1)} async-done(((f32[8,1,8]{2,1,0:T(1,128)}), f32[8,1,8]{2,1,0:T(1,128)S(1)}, u32[]{:S(2)}, u32[]{:S(2)}) %all-to-all-start.1) | async-done | bytes 288 | tf_op jit(solution)/shard_map/while/body/eval_jaxpr/all_to_all | solution.py:32
  211.7 4.5 %collective-permute-start.3 = (f32[4,8,4,1]{3,1,2,0:T(8,128)S(1)}, f32[4,8,4,1]{3,1,2,0:T(8,128)S(1)}, u32[]{:S(2)}, u32[]{:S(2)}) collective-permute-start(f32[4,8,4,1]{3,1,2,0:T(8,128)S(1)} %get-tuple-element.765), channel_id=1, source_target_pairs={{1,0},{2,1},{3,2},{4,3},{5,4},{6,5},{7,6},{8,7},{9,8},{10,9},{11,1... | collective-permute-start | bytes 1544 | tf_op jit(solution)/shard_map/while/body/eval_jaxpr/ppermute | solution.py:25
  223.4 6.4 %all-to-all-start = ((f32[32,1,8]{2,1,0:T(1,128)}), f32[32,1,8]{2,1,0:T(1,128)S(1)}, u32[]{:S(2)}, u32[]{:S(2)}) async-start(f32[32,1,8]{2,1,0:T(1,128)} %broadcast_in_dim.147), calls=%async_computation | async-start | bytes 32768 | tf_op jit(solution)/shard_map/while/body/eval_jaxpr/all_to_all | solution.py:32
  229.8 8.6 %all-to-all-done = f32[32,1,8]{2,1,0:T(1,128)S(1)} async-done(((f32[32,1,8]{2,1,0:T(1,128)}), f32[32,1,8]{2,1,0:T(1,128)S(1)}, u32[]{:S(2)}, u32[]{:S(2)}) %all-to-all-start) | async-done | bytes 1056 | tf_op jit(solution)/shard_map/while/body/eval_jaxpr/all_to_all | solution.py:32
  239.0 8.8 %all-to-all-start.1 = ((f32[8,1,8]{2,1,0:T(1,128)}), f32[8,1,8]{2,1,0:T(1,128)S(1)}, u32[]{:S(2)}, u32[]{:S(2)}) async-start(f32[8,1,8]{2,1,0:T(1,128)} %broadcast_in_dim.148), calls=%async_computation.1 | async-start | bytes 8192 | tf_op jit(solution)/shard_map/while/body/eval_jaxpr/all_to_all | solution.py:32
  247.9 4.5 %all-to-all-done.1 = f32[8,1,8]{2,1,0:T(1,128)S(1)} async-done(((f32[8,1,8]{2,1,0:T(1,128)}), f32[8,1,8]{2,1,0:T(1,128)S(1)}, u32[]{:S(2)}, u32[]{:S(2)}) %all-to-all-start.1) | async-done | bytes 288 | tf_op jit(solution)/shard_map/while/body/eval_jaxpr/all_to_all | solution.py:32
  258.6 3.8 %all-to-all-start.2 = ((f32[32,1,1]{2,1,0:T(1,128)}), f32[32,1,1]{2,1,0:T(1,128)S(1)}, u32[]{:S(2)}, u32[]{:S(2)}) async-start(f32[32,1,1]{2,1,0:T(1,128)} %broadcast_in_dim.113), calls=%async_computation.2 | async-start | bytes 32768 | tf_op jit(solution)/shard_map/all_to_all | solution.py:32
  262.9 8.1 %all-to-all-done.2 = f32[32,1,1]{2,1,0:T(1,128)S(1)} async-done(((f32[32,1,1]{2,1,0:T(1,128)}), f32[32,1,1]{2,1,0:T(1,128)S(1)}, u32[]{:S(2)}, u32[]{:S(2)}) %all-to-all-start.2) | async-done | bytes 160 | tf_op jit(solution)/shard_map/all_to_all | solution.py:32
  272.3 8.8 %all_to_all.46 = f32[8,1,1]{2,1,0:T(1,128)S(1)} all-to-all(f32[8,1,1]{2,1,0:T(1,128)S(1)} %broadcast_in_dim.114), channel_id=1, replica_groups=mesh['gx_0'=4,'gx_1'=2,'gy_0'=4,'gy_1'=8] {'gx_0','gx_1'}, dimensions={0} | all-to-all | bytes 64 | tf_op jit(solution)/shard_map/all_to_all | solution.py:32
  (309 shorter events, 77.0 us)
Async XLA Ops:
  2.2 12.7 %collective-permute-start.4 = (f32[4,8,1,128]{3,1,2,0:T(8,128)S(1)}, f32[4,8,1,128]{3,1,2,0:T(8,128)S(1)}, u32[]{:S(2)}, u32[]{:S(2)}) collective-permute-start(f32[4,8,1,128]{3,1,2,0:T(8,128)S(1)} %get-tuple-element.673), channel_id=1, source_target_pairs={{0,32},{32,64},{64,96},{96,128},{128,160},{160,192},{192,224},{224... | collective-permute-start | bytes 49160 | tf_op jit(solution)/shard_map/ppermute | solution.py:24
  4.9 10.2 %collective-permute-start.5 = (f32[4,8,1,128]{3,1,2,0:T(8,128)S(1)}, f32[4,8,1,128]{3,1,2,0:T(8,128)S(1)}, u32[]{:S(2)}, u32[]{:S(2)}) collective-permute-start(f32[4,8,1,128]{3,1,2,0:T(8,128)S(1)} %get-tuple-element.672), channel_id=1, source_target_pairs={{32,0},{64,32},{96,64},{128,96},{160,128},{192,160},{224,192},{0,2... | collective-permute-start | bytes 49160 | tf_op jit(solution)/shard_map/ppermute | solution.py:25
  6.2 9.1 %collective-permute-start.6 = (f32[4,8,4,1]{3,1,2,0:T(8,128)S(1)}, f32[4,8,4,1]{3,1,2,0:T(8,128)S(1)}, u32[]{:S(2)}, u32[]{:S(2)}) collective-permute-start(f32[4,8,4,1]{3,1,2,0:T(8,128)S(1)} %get-tuple-element.671), channel_id=1, source_target_pairs={{0,1},{1,2},{2,3},{3,4},{4,5},{5,6},{6,7},{7,8},{8,9},{9,10},{10,1... | collective-permute-start | bytes 1544 | tf_op jit(solution)/shard_map/ppermute | solution.py:24
  7.3 8.1 %collective-permute-start.7 = (f32[4,8,4,1]{3,1,2,0:T(8,128)S(1)}, f32[4,8,4,1]{3,1,2,0:T(8,128)S(1)}, u32[]{:S(2)}, u32[]{:S(2)}) collective-permute-start(f32[4,8,4,1]{3,1,2,0:T(8,128)S(1)} %get-tuple-element.670), channel_id=1, source_target_pairs={{1,0},{2,1},{3,2},{4,3},{5,4},{6,5},{7,6},{8,7},{9,8},{10,9},{11,1... | collective-permute-start | bytes 1544 | tf_op jit(solution)/shard_map/ppermute | solution.py:25
  17.7 8.6 %collective-permute-start = (f32[4,8,1,128]{3,1,2,0:T(8,128)S(1)}, f32[4,8,1,128]{3,1,2,0:T(8,128)S(1)}, u32[]{:S(2)}, u32[]{:S(2)}) collective-permute-start(f32[4,8,1,128]{3,1,2,0:T(8,128)S(1)} %get-tuple-element.757), channel_id=1, source_target_pairs={{0,32},{32,64},{64,96},{96,128},{128,160},{160,192},{192,224},{224... | collective-permute-start | bytes 49160 | tf_op jit(solution)/shard_map/while/body/eval_jaxpr/ppermute | solution.py:24
  20.2 6.3 %collective-permute-start.1 = (f32[4,8,1,128]{3,1,2,0:T(8,128)S(1)}, f32[4,8,1,128]{3,1,2,0:T(8,128)S(1)}, u32[]{:S(2)}, u32[]{:S(2)}) collective-permute-start(f32[4,8,1,128]{3,1,2,0:T(8,128)S(1)} %get-tuple-element.759), channel_id=1, source_target_pairs={{32,0},{64,32},{96,64},{128,96},{160,128},{192,160},{224,192},{0,2... | collective-permute-start | bytes 49160 | tf_op jit(solution)/shard_map/while/body/eval_jaxpr/ppermute | solution.py:25
  20.9 6.5 %collective-permute-start.2 = (f32[4,8,4,1]{3,1,2,0:T(8,128)S(1)}, f32[4,8,4,1]{3,1,2,0:T(8,128)S(1)}, u32[]{:S(2)}, u32[]{:S(2)}) collective-permute-start(f32[4,8,4,1]{3,1,2,0:T(8,128)S(1)} %get-tuple-element.763), channel_id=1, source_target_pairs={{0,1},{1,2},{2,3},{3,4},{4,5},{5,6},{6,7},{7,8},{8,9},{9,10},{10,1... | collective-permute-start | bytes 1544 | tf_op jit(solution)/shard_map/while/body/eval_jaxpr/ppermute | solution.py:24
  21.0 6.5 %collective-permute-start.3 = (f32[4,8,4,1]{3,1,2,0:T(8,128)S(1)}, f32[4,8,4,1]{3,1,2,0:T(8,128)S(1)}, u32[]{:S(2)}, u32[]{:S(2)}) collective-permute-start(f32[4,8,4,1]{3,1,2,0:T(8,128)S(1)} %get-tuple-element.765), channel_id=1, source_target_pairs={{1,0},{2,1},{3,2},{4,3},{5,4},{6,5},{7,6},{8,7},{9,8},{10,9},{11,1... | collective-permute-start | bytes 1544 | tf_op jit(solution)/shard_map/while/body/eval_jaxpr/ppermute | solution.py:25
  33.0 15.0 %all-to-all-start = ((f32[32,1,8]{2,1,0:T(1,128)}), f32[32,1,8]{2,1,0:T(1,128)S(1)}, u32[]{:S(2)}, u32[]{:S(2)}) async-start(f32[32,1,8]{2,1,0:T(1,128)} %broadcast_in_dim.147), calls=%async_computation | async-start | bytes 32768 | tf_op jit(solution)/shard_map/while/body/eval_jaxpr/all_to_all | solution.py:32
  48.6 13.5 %all-to-all-start.1 = ((f32[8,1,8]{2,1,0:T(1,128)}), f32[8,1,8]{2,1,0:T(1,128)S(1)}, u32[]{:S(2)}, u32[]{:S(2)}) async-start(f32[8,1,8]{2,1,0:T(1,128)} %broadcast_in_dim.148), calls=%async_computation.1 | async-start | bytes 8192 | tf_op jit(solution)/shard_map/while/body/eval_jaxpr/all_to_all | solution.py:32
  67.1 7.0 %collective-permute-start = (f32[4,8,1,128]{3,1,2,0:T(8,128)S(1)}, f32[4,8,1,128]{3,1,2,0:T(8,128)S(1)}, u32[]{:S(2)}, u32[]{:S(2)}) collective-permute-start(f32[4,8,1,128]{3,1,2,0:T(8,128)S(1)} %get-tuple-element.757), channel_id=1, source_target_pairs={{0,32},{32,64},{64,96},{96,128},{128,160},{160,192},{192,224},{224... | collective-permute-start | bytes 49160 | tf_op jit(solution)/shard_map/while/body/eval_jaxpr/ppermute | solution.py:24
  67.9 6.3 %collective-permute-start.1 = (f32[4,8,1,128]{3,1,2,0:T(8,128)S(1)}, f32[4,8,1,128]{3,1,2,0:T(8,128)S(1)}, u32[]{:S(2)}, u32[]{:S(2)}) collective-permute-start(f32[4,8,1,128]{3,1,2,0:T(8,128)S(1)} %get-tuple-element.759), channel_id=1, source_target_pairs={{32,0},{64,32},{96,64},{128,96},{160,128},{192,160},{224,192},{0,2... | collective-permute-start | bytes 49160 | tf_op jit(solution)/shard_map/while/body/eval_jaxpr/ppermute | solution.py:25
  68.6 6.5 %collective-permute-start.2 = (f32[4,8,4,1]{3,1,2,0:T(8,128)S(1)}, f32[4,8,4,1]{3,1,2,0:T(8,128)S(1)}, u32[]{:S(2)}, u32[]{:S(2)}) collective-permute-start(f32[4,8,4,1]{3,1,2,0:T(8,128)S(1)} %get-tuple-element.763), channel_id=1, source_target_pairs={{0,1},{1,2},{2,3},{3,4},{4,5},{5,6},{6,7},{7,8},{8,9},{9,10},{10,1... | collective-permute-start | bytes 1544 | tf_op jit(solution)/shard_map/while/body/eval_jaxpr/ppermute | solution.py:24
  69.0 6.2 %collective-permute-start.3 = (f32[4,8,4,1]{3,1,2,0:T(8,128)S(1)}, f32[4,8,4,1]{3,1,2,0:T(8,128)S(1)}, u32[]{:S(2)}, u32[]{:S(2)}) collective-permute-start(f32[4,8,4,1]{3,1,2,0:T(8,128)S(1)} %get-tuple-element.765), channel_id=1, source_target_pairs={{1,0},{2,1},{3,2},{4,3},{5,4},{6,5},{7,6},{8,7},{9,8},{10,9},{11,1... | collective-permute-start | bytes 1544 | tf_op jit(solution)/shard_map/while/body/eval_jaxpr/ppermute | solution.py:25
  80.7 15.0 %all-to-all-start = ((f32[32,1,8]{2,1,0:T(1,128)}), f32[32,1,8]{2,1,0:T(1,128)S(1)}, u32[]{:S(2)}, u32[]{:S(2)}) async-start(f32[32,1,8]{2,1,0:T(1,128)} %broadcast_in_dim.147), calls=%async_computation | async-start | bytes 32768 | tf_op jit(solution)/shard_map/while/body/eval_jaxpr/all_to_all | solution.py:32
  96.3 13.4 %all-to-all-start.1 = ((f32[8,1,8]{2,1,0:T(1,128)}), f32[8,1,8]{2,1,0:T(1,128)S(1)}, u32[]{:S(2)}, u32[]{:S(2)}) async-start(f32[8,1,8]{2,1,0:T(1,128)} %broadcast_in_dim.148), calls=%async_computation.1 | async-start | bytes 8192 | tf_op jit(solution)/shard_map/while/body/eval_jaxpr/all_to_all | solution.py:32
  114.6 7.0 %collective-permute-start = (f32[4,8,1,128]{3,1,2,0:T(8,128)S(1)}, f32[4,8,1,128]{3,1,2,0:T(8,128)S(1)}, u32[]{:S(2)}, u32[]{:S(2)}) collective-permute-start(f32[4,8,1,128]{3,1,2,0:T(8,128)S(1)} %get-tuple-element.757), channel_id=1, source_target_pairs={{0,32},{32,64},{64,96},{96,128},{128,160},{160,192},{192,224},{224... | collective-permute-start | bytes 49160 | tf_op jit(solution)/shard_map/while/body/eval_jaxpr/ppermute | solution.py:24
  115.5 6.3 %collective-permute-start.1 = (f32[4,8,1,128]{3,1,2,0:T(8,128)S(1)}, f32[4,8,1,128]{3,1,2,0:T(8,128)S(1)}, u32[]{:S(2)}, u32[]{:S(2)}) collective-permute-start(f32[4,8,1,128]{3,1,2,0:T(8,128)S(1)} %get-tuple-element.759), channel_id=1, source_target_pairs={{32,0},{64,32},{96,64},{128,96},{160,128},{192,160},{224,192},{0,2... | collective-permute-start | bytes 49160 | tf_op jit(solution)/shard_map/while/body/eval_jaxpr/ppermute | solution.py:25
  116.2 6.5 %collective-permute-start.2 = (f32[4,8,4,1]{3,1,2,0:T(8,128)S(1)}, f32[4,8,4,1]{3,1,2,0:T(8,128)S(1)}, u32[]{:S(2)}, u32[]{:S(2)}) collective-permute-start(f32[4,8,4,1]{3,1,2,0:T(8,128)S(1)} %get-tuple-element.763), channel_id=1, source_target_pairs={{0,1},{1,2},{2,3},{3,4},{4,5},{5,6},{6,7},{7,8},{8,9},{9,10},{10,1... | collective-permute-start | bytes 1544 | tf_op jit(solution)/shard_map/while/body/eval_jaxpr/ppermute | solution.py:24
  128.3 15.0 %all-to-all-start = ((f32[32,1,8]{2,1,0:T(1,128)}), f32[32,1,8]{2,1,0:T(1,128)S(1)}, u32[]{:S(2)}, u32[]{:S(2)}) async-start(f32[32,1,8]{2,1,0:T(1,128)} %broadcast_in_dim.147), calls=%async_computation | async-start | bytes 32768 | tf_op jit(solution)/shard_map/while/body/eval_jaxpr/all_to_all | solution.py:32
  143.9 13.4 %all-to-all-start.1 = ((f32[8,1,8]{2,1,0:T(1,128)}), f32[8,1,8]{2,1,0:T(1,128)S(1)}, u32[]{:S(2)}, u32[]{:S(2)}) async-start(f32[8,1,8]{2,1,0:T(1,128)} %broadcast_in_dim.148), calls=%async_computation.1 | async-start | bytes 8192 | tf_op jit(solution)/shard_map/while/body/eval_jaxpr/all_to_all | solution.py:32
  162.2 7.0 %collective-permute-start = (f32[4,8,1,128]{3,1,2,0:T(8,128)S(1)}, f32[4,8,1,128]{3,1,2,0:T(8,128)S(1)}, u32[]{:S(2)}, u32[]{:S(2)}) collective-permute-start(f32[4,8,1,128]{3,1,2,0:T(8,128)S(1)} %get-tuple-element.757), channel_id=1, source_target_pairs={{0,32},{32,64},{64,96},{96,128},{128,160},{160,192},{192,224},{224... | collective-permute-start | bytes 49160 | tf_op jit(solution)/shard_map/while/body/eval_jaxpr/ppermute | solution.py:24
  163.1 6.3 %collective-permute-start.1 = (f32[4,8,1,128]{3,1,2,0:T(8,128)S(1)}, f32[4,8,1,128]{3,1,2,0:T(8,128)S(1)}, u32[]{:S(2)}, u32[]{:S(2)}) collective-permute-start(f32[4,8,1,128]{3,1,2,0:T(8,128)S(1)} %get-tuple-element.759), channel_id=1, source_target_pairs={{32,0},{64,32},{96,64},{128,96},{160,128},{192,160},{224,192},{0,2... | collective-permute-start | bytes 49160 | tf_op jit(solution)/shard_map/while/body/eval_jaxpr/ppermute | solution.py:25
  163.8 6.5 %collective-permute-start.2 = (f32[4,8,4,1]{3,1,2,0:T(8,128)S(1)}, f32[4,8,4,1]{3,1,2,0:T(8,128)S(1)}, u32[]{:S(2)}, u32[]{:S(2)}) collective-permute-start(f32[4,8,4,1]{3,1,2,0:T(8,128)S(1)} %get-tuple-element.763), channel_id=1, source_target_pairs={{0,1},{1,2},{2,3},{3,4},{4,5},{5,6},{6,7},{7,8},{8,9},{9,10},{10,1... | collective-permute-start | bytes 1544 | tf_op jit(solution)/shard_map/while/body/eval_jaxpr/ppermute | solution.py:24
  175.9 15.0 %all-to-all-start = ((f32[32,1,8]{2,1,0:T(1,128)}), f32[32,1,8]{2,1,0:T(1,128)S(1)}, u32[]{:S(2)}, u32[]{:S(2)}) async-start(f32[32,1,8]{2,1,0:T(1,128)} %broadcast_in_dim.147), calls=%async_computation | async-start | bytes 32768 | tf_op jit(solution)/shard_map/while/body/eval_jaxpr/all_to_all | solution.py:32
  191.5 13.4 %all-to-all-start.1 = ((f32[8,1,8]{2,1,0:T(1,128)}), f32[8,1,8]{2,1,0:T(1,128)S(1)}, u32[]{:S(2)}, u32[]{:S(2)}) async-start(f32[8,1,8]{2,1,0:T(1,128)} %broadcast_in_dim.148), calls=%async_computation.1 | async-start | bytes 8192 | tf_op jit(solution)/shard_map/while/body/eval_jaxpr/all_to_all | solution.py:32
  209.8 7.0 %collective-permute-start = (f32[4,8,1,128]{3,1,2,0:T(8,128)S(1)}, f32[4,8,1,128]{3,1,2,0:T(8,128)S(1)}, u32[]{:S(2)}, u32[]{:S(2)}) collective-permute-start(f32[4,8,1,128]{3,1,2,0:T(8,128)S(1)} %get-tuple-element.757), channel_id=1, source_target_pairs={{0,32},{32,64},{64,96},{96,128},{128,160},{160,192},{192,224},{224... | collective-permute-start | bytes 49160 | tf_op jit(solution)/shard_map/while/body/eval_jaxpr/ppermute | solution.py:24
  210.7 6.3 %collective-permute-start.1 = (f32[4,8,1,128]{3,1,2,0:T(8,128)S(1)}, f32[4,8,1,128]{3,1,2,0:T(8,128)S(1)}, u32[]{:S(2)}, u32[]{:S(2)}) collective-permute-start(f32[4,8,1,128]{3,1,2,0:T(8,128)S(1)} %get-tuple-element.759), channel_id=1, source_target_pairs={{32,0},{64,32},{96,64},{128,96},{160,128},{192,160},{224,192},{0,2... | collective-permute-start | bytes 49160 | tf_op jit(solution)/shard_map/while/body/eval_jaxpr/ppermute | solution.py:25
  211.3 6.5 %collective-permute-start.2 = (f32[4,8,4,1]{3,1,2,0:T(8,128)S(1)}, f32[4,8,4,1]{3,1,2,0:T(8,128)S(1)}, u32[]{:S(2)}, u32[]{:S(2)}) collective-permute-start(f32[4,8,4,1]{3,1,2,0:T(8,128)S(1)} %get-tuple-element.763), channel_id=1, source_target_pairs={{0,1},{1,2},{2,3},{3,4},{4,5},{5,6},{6,7},{7,8},{8,9},{9,10},{10,1... | collective-permute-start | bytes 1544 | tf_op jit(solution)/shard_map/while/body/eval_jaxpr/ppermute | solution.py:24
  223.4 15.0 %all-to-all-start = ((f32[32,1,8]{2,1,0:T(1,128)}), f32[32,1,8]{2,1,0:T(1,128)S(1)}, u32[]{:S(2)}, u32[]{:S(2)}) async-start(f32[32,1,8]{2,1,0:T(1,128)} %broadcast_in_dim.147), calls=%async_computation | async-start | bytes 32768 | tf_op jit(solution)/shard_map/while/body/eval_jaxpr/all_to_all | solution.py:32
  239.0 13.4 %all-to-all-start.1 = ((f32[8,1,8]{2,1,0:T(1,128)}), f32[8,1,8]{2,1,0:T(1,128)S(1)}, u32[]{:S(2)}, u32[]{:S(2)}) async-start(f32[8,1,8]{2,1,0:T(1,128)} %broadcast_in_dim.148), calls=%async_computation.1 | async-start | bytes 8192 | tf_op jit(solution)/shard_map/while/body/eval_jaxpr/all_to_all | solution.py:32
  258.6 12.4 %all-to-all-start.2 = ((f32[32,1,1]{2,1,0:T(1,128)}), f32[32,1,1]{2,1,0:T(1,128)S(1)}, u32[]{:S(2)}, u32[]{:S(2)}) async-start(f32[32,1,1]{2,1,0:T(1,128)} %broadcast_in_dim.113), calls=%async_computation.2 | async-start | bytes 32768 | tf_op jit(solution)/shard_map/all_to_all | solution.py:32
  (10 other events, 42.5 us)
where the time goes:
time: 284 us; the launch traced here: 283 us
  starting transfers between devices  121 us (43%)
  waiting for transfers between devices  77.4 us (27%)
  matrix products  30.1 us (11%)
  other arithmetic  19.2 us (7%)
  local copies, waits for them, and re-layouts  17.2 us (6%)
  blocking collectives  8.79 us (3%)
  loops' own time  8.09 us (3%)
    all_to_all x11, starting transfers between devices, sent_to_all(): return lax.all_to_all(copies, axis, split_axis=0, concat_axis=0, tiled=True)  80 us
    all_to_all x11, waiting for transfers between devices, sent_to_all(): return lax.all_to_all(copies, axis, split_axis=0, concat_axis=0, tiled=True)  73.7 us
    ppermute x12, starting transfers between devices, extended(): after = lax.ppermute(leading, axis, down)  29.4 us
    dot_general x5, matrix products, products(): per_cell = jnp.einsum('kqxy,qxy->kxy', basis, image, precision=highest)  13.2 us
    ppermute x12, starting transfers between devices, extended(): before = lax.ppermute(last, axis, up)  11.4 us
    all_to_all x1, blocking collectives, sent_to_all(): return lax.all_to_all(copies, axis, split_axis=0, concat_axis=0, tiled=True)  8.79 us
    reduce_sum x12, other arithmetic, local_total(): return jnp.sum(jnp.sum(values, axis=0))  8.12 us
    another operation x1, loops' own time, body(): lax.fori_loop(0, ITERS, advance, (basis, hessen, first))  8.09 us
  transfers between devices with their start and end apart: 35, of which 16 were waited for; matrix products, arithmetic and copies ran while one was open for 3% of the time, Pallas kernels for 0%

commit v1 on v0

v1 whole, which is shorter than its diff:
```python
import functools

import jax
import jax.numpy as jnp
from jax import lax
from jax.experimental import pallas as pl
from jax.experimental.pallas import tpu as pltpu
from jax.sharding import Mesh
from jax.sharding import PartitionSpec as P

P_SIZE = 8
ITERS = 5
NV = ITERS + 1
TAU = 2.0
FLOOR = 0.1
MESH = pl.DeviceIdType.MESH
AXES = ("y", "c", "x", "z")
PAIRS = [(i, j) for j in range(NV) for i in range(j + 1)]


def two_sum(a, b):
    s = a + b
    t = s - a
    return s, (a - (s - t)) + (b - t)


def quick(a, b):
    s = a + b
    return s, b - (s - a)


def split(a):
    c = a * 4097.0
    hi = c - (c - a)
    return hi, a - hi


def two_prod(a, b):
    p = a * b
    ah, al = split(a)
    bh, bl = split(b)
    return p, ((ah * bh - p) + ah * bl + al * bh) + al * bl


def add2(a, b):
    s, e = two_sum(a[0], b[0])
    return quick(s, e + (a[1] + b[1]))


def mul2(a, b):
    p, e = two_prod(a[0], b[0])
    return quick(p, e + (a[0] * b[1] + a[1] * b[0]))


def mul1(a, b):
    p, e = two_prod(a[0], b)
    return quick(p, e + a[1] * b)


def tree(items, op):
    items = list(items)
    while len(items) > 1:
        nxt = [op(items[i], items[i + 1]) for i in range(0, len(items) - 1, 2)]
        if len(items) % 2:
            nxt.append(items[-1])
        items = nxt
    return items[0]


def sublane_total(a):
    for s in (4, 2, 1):
        a = add2(a, tuple(pltpu.roll(v, s, 0) for v in a))
    return a


def kernel(sizes, line, fd, src_h, x0_h, rx_h, st_h, wf_h, hess, out_h,
           srcv, xin, rxin, stin, wfin, w, rx, st, op, qf, sxy, rxy, row1, buf1, row2, buf2, vout,
           lsem, osem, hs, hr, s1, r1, s2, r2):
    ny, nc, nx, nz = sizes
    y, c, x, z = (lax.axis_index(a) for a in AXES)

    def gx(s):
        g = lax.rem(y * nc + c + ny * nc + s, ny * nc)
        return (g // nc, lax.rem(g, nc), x, z)

    def gy(s):
        g = lax.rem(x * nz + z + nx * nz + s, nx * nz)
        return (y, c, g // nz, lax.rem(g, nz))

    east, west, north, south = gx(1), gx(-1), gy(1), gy(-1)
    group1 = [
        (lax.rem(y + i, ny), lax.rem(c + j, nc), lax.rem(x + k, nx), z)
        for i in range(ny) for j in range(nc) for k in range(nx) if i + j + k > 0
    ]
    group2 = [(y, c, x, lax.rem(z + k, nz)) for k in range(1, nz)]
    barrier = pltpu.get_barrier_semaphore()
    greeted = [east, west, north, south] + group1 + group2
    for peer in greeted:
        pl.semaphore_signal(barrier, inc=1, device_id=peer, device_id_type=MESH)
    loads = [
        pltpu.make_async_copy(a, b, lsem.at[i])
        for i, (a, b) in enumerate([(x0_h, xin), (rx_h, rxin), (src_h, srcv), (st_h, stin), (wf_h, wfin)])
    ]
    for cp in loads:
        cp.start()

    n = P_SIZE
    total = float(ny * nc * nx * nz * src_h.shape[0] * src_h.shape[1] * src_h.shape[2])
    lop = [[line[i, j] for j in range(n)] for i in range(n)]
    g = [0.5 * fd[i] + (TAU if i == 0 else 0.0) for i in range(n)]
    diag = lop[0][0]
    for i in range(1, n):
        diag = diag + lop[i][i]
    shift = 3.0 + 0.3125 * diag + 0.25 * fd[0]

    lane = lax.broadcasted_iota(jnp.int32, (8, 128), 1)
    sub = lax.broadcasted_iota(jnp.int32, (8, 128), 0)
    group = lane // 16
    zero4 = jnp.zeros((4, 128), jnp.float32)
    for cp in loads:
        cp.wait()
    for q in range(n * n):
        w[0, q, 0:4, :] = xin[q]
        w[0, q, 4:8, :] = zero4
        rx[q, 0:4, :] = rxin[q] - shift
        rx[q, 4:8, :] = zero4
    st[0:4, :] = stin[...]
    st[4:8, :] = zero4
    for f in range(4):
        op[f, 0:4, :] = 1.0 - wfin[f].astype(jnp.float32)
        op[f, 4:8, :] = zero4
    pl.semaphore_wait(barrier, len(greeted))

    def apply(k):
        def v(a, b):
            return w[k, a * n + b]

        pn = ps = jnp.zeros((8, 128), jnp.float32)
        for a in range(n):
            qs = tree([g[i] * v(a, i) for i in range(n)], jnp.add)
            qn = tree([g[i] * v(a, n - 1 - i) for i in range(n)], jnp.add)
            qf[2, a] = qs
            qf[3, a] = qn
            pn = jnp.where(group == a, pltpu.roll(qn, (16 * a + 1) % 128, 1), pn)
            ps = jnp.where(group == a, pltpu.roll(qs, 16 * a, 1), ps)
        sxy[k, 2] = ps
        sxy[k, 3] = pn
        for b in range(n):
            qw = tree([g[i] * v(i, b) for i in range(n)], jnp.add)
            qe = tree([g[i] * v(n - 1 - i, b) for i in range(n)], jnp.add)
            qf[0, b] = qw
            qf[1, b] = qe
            sxy[k, 0, pl.ds(b, 1), :] = qw[0:1, :]
            sxy[k, 1, pl.ds(b, 1), :] = qe[3:4, :]
        copies = []
        for f, peer in ((3, north), (2, south), (1, east), (0, west)):
            cp = pltpu.make_async_remote_copy(
                src_ref=sxy.at[k, f], dst_ref=rxy.at[k, f], send_sem=hs.at[k, f], recv_sem=hr.at[k, f],
                device_id=peer, device_id_type=MESH)
            cp.start()
            copies.append(cp)
        stiff = st[...]
        for b in range(n):
            col = [v(i, b) for i in range(n)]
            for a in range(n):
                acc = tree([lop[a][i] * col[i] for i in range(n)] + [lop[b][i] * v(a, i) for i in range(n)], jnp.add)
                w[k + 1, a * n + b] = rx[a * n + b] * col[a] + stiff * acc
        for cp in copies:
            cp.wait()
        for b in range(n):
            before = jnp.where(sub == 0, jnp.broadcast_to(rxy[k, 1, pl.ds(b, 1), :], (8, 128)), pltpu.roll(qf[1, b], 1, 0))
            after = jnp.where(sub == 3, jnp.broadcast_to(rxy[k, 0, pl.ds(b, 1), :], (8, 128)), pltpu.roll(qf[0, b], 7, 0))
            w[k + 1, b] = w[k + 1, b] + (qf[0, b] - op[0] * before)
            w[k + 1, 7 * n + b] = w[k + 1, 7 * n + b] + (qf[1, b] - op[1] * after)
        rn = rxy[k, 3]
        rs = rxy[k, 2]
        for a in range(n):
            before = jnp.where(lane == 0, pltpu.roll(rn, (128 - 16 * a) % 128, 1), pltpu.roll(qf[3, a], 1, 1))
            after = jnp.where(lane == 127, pltpu.roll(rs, (127 - 16 * a) % 128, 1), pltpu.roll(qf[2, a], 127, 1))
            w[k + 1, a * n] = w[k + 1, a * n] + (qf[2, a] - op[2] * before)
            w[k + 1, a * n + 7] = w[k + 1, a * n + 7] + (qf[3, a] - op[3] * after)

    apply(0)
    for q in range(n * n):
        w[1, q, 0:4, :] = w[1, q, 0:4, :] - (srcv[q] - shift * xin[q])

    def step(k, carry):
        apply(k)
        return carry

    lax.fori_loop(1, NV, step, 0)

    def gram(q, acc):
        vals = [w[i + 1, q] for i in range(NV)]
        return tuple(t + vals[i] * vals[j] for t, (i, j) in zip(acc, PAIRS))

    acc = lax.fori_loop(0, n * n, gram, tuple(jnp.zeros((8, 128), jnp.float32) for _ in PAIRS))
    line_row = jnp.zeros((8, 128), jnp.float32)
    for base in range(0, len(PAIRS), 8):
        packed = jnp.zeros((8, 128), jnp.float32)
        for i, t in enumerate(acc[base:base + 8]):
            t = jnp.where(sub < 4, t, 0.0)
            t = t + pltpu.roll(t, 4, 0)
            t = t + pltpu.roll(t, 2, 0)
            t = t + pltpu.roll(t, 1, 0)
            packed = jnp.where(sub == i, t, packed)
        packed = jnp.sum(packed, axis=1, keepdims=True) * (1.0 / total)
        line_row = line_row + jnp.where(lane == sub + base, packed, 0.0)
    for s in (4, 2, 1):
        line_row = line_row + pltpu.roll(line_row, s, 0)
    row1[...] = line_row[0:1, :]
    copies = []
    for j, peer in enumerate(group1):
        cp = pltpu.make_async_remote_copy(
            src_ref=row1, dst_ref=buf1.at[j], send_sem=s1.at[j], recv_sem=r1.at[j], device_id=peer, device_id_type=MESH)
        cp.start()
        copies.append(cp)
    for cp in copies:
        cp.wait()
    zero1 = jnp.zeros((1, 128), jnp.float32)
    part = tree([(row1[...], zero1)] + [(buf1[j], zero1) for j in range(len(group1))], add2)
    row2[0:1, :] = part[0]
    row2[1:2, :] = part[1]
    copies = []
    for j, peer in enumerate(group2):
        cp = pltpu.make_async_remote_copy(
            src_ref=row2, dst_ref=buf2.at[j], send_sem=s2.at[j], recv_sem=r2.at[j], device_id=peer, device_id_type=MESH)
        cp.start()
        copies.append(cp)
    for cp in copies:
        cp.wait()
    part = tree([part] + [(buf2[j, 0:1, :], buf2[j, 1:2, :]) for j in range(len(group2))], add2)

    slot = {}
    for p, (i, j) in enumerate(PAIRS):
        slot[i, j] = slot[j, i] = p
    columns = []
    for k in range(NV):
        at = jnp.full((8, 128), -1, jnp.int32)
        for i in range(NV):
            at = jnp.where(sub == i, slot[i, k], at)
        columns.append(tuple(
            jnp.broadcast_to(
                jnp.sum(jnp.where(lane == at, jnp.broadcast_to(t, (8, 128)), 0.0), axis=1, keepdims=True), (8, 128))
            for t in part))

    def spread(t, k):
        return jnp.broadcast_to(t[k:k + 1, :], (8, 128))

    def times_gram(u):
        return tree([mul2(columns[k], tuple(spread(t, k) for t in u)) for k in range(NV)], add2)

    def dot(a, b):
        return sublane_total(mul2(a, b))

    hmat = jnp.zeros((8, 128), jnp.float32)
    zeros = jnp.zeros((8, 128), jnp.float32)
    u = (jnp.where(sub == 0, -1.0, 0.0), zeros)
    e = times_gram(u)
    coefs, images = [], []
    for j in range(NV):
        square = dot(u, e)[0] + FLOOR
        inv = lax.rsqrt(square)
        if j > 0:
            hmat = jnp.where((sub == j) & (lane == j - 1), square * inv, hmat)
        coefs.append(mul1(u, inv))
        images.append(mul1(e, inv))
        if j == ITERS:
            break
        moved = tuple(pltpu.roll(t, 1, 0) for t in coefs[j])
        u = add2(moved, mul1(coefs[j], jnp.broadcast_to(shift, (8, 128))))
        e = times_gram(u)
        hs_j = [dot(images[i], u)[0] for i in range(j + 1)]
        for i in range(j + 1):
            hmat = jnp.where((sub == i) & (lane == j), hs_j[i], hmat)
        u = tree([u] + [mul1(coefs[i], -hs_j[i]) for i in range(j + 1)], add2)
        e = tree([e] + [mul1(images[i], -hs_j[i]) for i in range(j + 1)], add2)
    hess[...] = hmat[0:NV, 0:ITERS]

    weights = [[jnp.broadcast_to(coefs[j][0][i:i + 1, :], (8, 128)) for i in range(j + 1)] for j in range(NV)]

    outs = []
    for j in range(NV):
        def combine(q, carry, j=j):
            t = tree([weights[j][i] * w[i + 1, q] for i in range(j + 1)], jnp.add)
            vout[j, q] = t[0:4, :]
            return carry

        lax.fori_loop(0, n * n, combine, 0, unroll=8)
        cp = pltpu.make_async_copy(vout.at[j], out_h.at[j], osem.at[j])
        cp.start()
        outs.append(cp)
    for cp in outs:
        cp.wait()


def solution(mesh):
    ny, nc, nx, nz = 4, 2, 4, 8
    finer = Mesh(mesh.devices.reshape(ny, nc, nx, nz), AXES)
    gxs, gys = ("y", "c"), ("x", "z")
    sizes = (ny, nc, nx, nz)
    f32 = jnp.float32

    def body(source, initial, reaction, stiffness, line_op, face_deriv, wall_flags):
        nodes, ex, ey = source.shape
        n1, n2 = ny * nc * nx - 1, nz - 1
        anywhere = pl.BlockSpec(memory_space=pl.ANY)
        scalars = pl.BlockSpec(memory_space=pltpu.SMEM)
        vm = pltpu.VMEM
        dma = pltpu.SemaphoreType.DMA
        return pl.pallas_call(
            functools.partial(kernel, sizes),
            out_shape=(
                jax.ShapeDtypeStruct((NV, ITERS), f32),
                jax.ShapeDtypeStruct((NV, nodes, ex, ey), f32),
            ),
            in_specs=[scalars, scalars] + [anywhere] * 5,
            out_specs=(pl.BlockSpec(memory_space=pltpu.VMEM), anywhere),
            scratch_shapes=[
                vm((nodes, ex, ey), f32), vm((nodes, ex, ey), f32), vm((nodes, ex, ey), f32),
                vm((ex, ey), f32), vm((4, ex, ey), jnp.int32),
                vm((NV + 1, nodes, 8, ey), f32), vm((nodes, 8, ey), f32), vm((8, ey), f32), vm((4, 8, ey), f32),
                vm((4, 8, 8, ey), f32),
                vm((NV, 4, 8, ey), f32), vm((NV, 4, 8, ey), f32),
                vm((1, 128), f32), vm((n1, 1, 128), f32), vm((2, 128), f32), vm((n2, 2, 128), f32),
                vm((NV, nodes, ex, ey), f32),
                dma((5,)), dma((NV,)), dma((NV, 4)), dma((NV, 4)), dma((n1,)), dma((n1,)), dma((n2,)), dma((n2,)),
            ],
            compiler_params=pltpu.CompilerParams(
                collective_id=0, has_side_effects=True, vmem_limit_bytes=48 * 1024 * 1024),
            name="arnoldi",
        )(line_op, face_deriv, source, initial, reaction, stiffness, wall_flags)

    placed = (P(None, gxs, gys), P(None, gxs, gys), P(None, gxs, gys), P(gxs, gys), P(), P(), P(None, gxs, gys))
    return jax.shard_map(
        body, mesh=finer, in_specs=placed, out_specs=(P(), P(None, None, gxs, gys)), check_vma=False)
```

time: 284 us -> 57.6 us (0.20)
  starting transfers between devices: 121 us -> 0 us
  waiting for transfers between devices: 77.4 us -> 0 us
  Pallas kernels: 0 us -> 49.8 us
  matrix products: 30.1 us -> 0 us
  other arithmetic: 19.2 us -> 0 us
  local copies, waits for them, and re-layouts: 17.2 us -> 6.9 us
  blocking collectives: 8.79 us -> 0 us
  loops' own time: 8.09 us -> 0 us
    all_to_all x11 -> x0, starting transfers between devices: 80 us -> none  [sent_to_all(): return lax.all_to_all(copies, axis, split_axis=0, concat_axis=0, tiled=True)]
    all_to_all x11 -> x0, waiting for transfers between devices: 73.7 us -> none  [sent_to_all(): return lax.all_to_all(copies, axis, split_axis=0, concat_axis=0, tiled=True)]
    pallas_call x0 -> x1, Pallas kernels: none -> 49.8 us  [body(): pl.pallas_call(functools.partial(kernel, sizes), out_shape=(jax.ShapeDtyp...]
    ppermute x24 -> x0, starting transfers between devices: 40.9 us -> none  [the longest x12 29.4 us: extended(): after = lax.ppermute(leading, axis, down)]
    dot_general x46 -> x0, matrix products: 30.1 us -> none  [the longest x5 13.2 us: products(): per_cell = jnp.einsum('kqxy,qxy->kxy', basis, image, precision=highest)]
    reduce_sum x24 -> x0, other arithmetic: 9.72 us -> none  [the longest x12 8.12 us: local_total(): return jnp.sum(jnp.sum(values, axis=0))]
    all_to_all x1 -> x0, blocking collectives: 8.79 us -> none  [sent_to_all(): return lax.all_to_all(copies, axis, split_axis=0, concat_axis=0, tiled=True)]
    another operation x1 -> x0, loops' own time: 8.09 us -> none  [body(): lax.fori_loop(0, ITERS, advance, (basis, hessen, first))]
  transfers between devices with their start and end apart: 35 -> 0, of which waited for: 16 -> 0; matrix products, arithmetic and copies ran while one was open for 3% -> 0% of each run, Pallas kernels for 0% -> 0%
where the time goes in v1:
time: 57.6 us; the launch traced here: 57.3 us
  Pallas kernels  49.8 us (86%)
  local copies, waits for them, and re-layouts  6.9 us (12%)
  between operations  0.66 us (1%)
    pallas_call x1, Pallas kernels, body(): pl.pallas_call(functools.partial(kernel, sizes), out_shape=(jax.ShapeDtyp...  49.8 us
    unnamed x16, local copies, waits for them, and re-layouts  6.9 us

profile of v1, /device:TPU:1, one launch (start us, length us, event | category | flops | bytes accessed | tf_op | source)
XLA Modules:
  0.0 57.3 jit_solution(10234126361449844536)
XLA Ops:
  0.6 0.0 copy-start
  0.6 0.9 %copy-done = f32[64,4,128]{2,1,0:T(4,128)S(1)} copy-done((f32[64,4,128]{2,1,0:T(4,128)S(1)}, f32[64,4,128]{2,1,0:T(4,128)}, u32[]{:S(2)}) %copy-start) | copy-done | bytes 131096
  1.5 0.0 copy-start.1
  1.5 0.9 %copy-done.1 = f32[64,4,128]{2,1,0:T(4,128)S(1)} copy-done((f32[64,4,128]{2,1,0:T(4,128)S(1)}, f32[64,4,128]{2,1,0:T(4,128)}, u32[]{:S(2)}) %copy-start.1) | copy-done | bytes 131096
  2.4 0.0 copy-start.2
  2.4 0.9 %copy-done.2 = f32[64,4,128]{2,1,0:T(4,128)S(1)} copy-done((f32[64,4,128]{2,1,0:T(4,128)S(1)}, f32[64,4,128]{2,1,0:T(4,128)}, u32[]{:S(2)}) %copy-start.2) | copy-done | bytes 131096
  3.3 0.0 copy-start.3
  3.3 0.7 %copy-done.3 = s32[4,4,128]{2,1,0:T(4,128)S(1)} copy-done((s32[4,4,128]{2,1,0:T(4,128)S(1)}, s32[4,4,128]{2,1,0:T(4,128)}, u32[]{:S(2)}) %copy-start.3) | copy-done | bytes 8216
  4.0 0.0 copy-start.4
  4.0 0.7 %copy-done.4 = f32[8,8]{1,0:T(8,128)S(1)} copy-done((f32[8,8]{1,0:T(8,128)S(1)}, f32[8,8]{1,0:T(8,128)}, u32[]{:S(2)}) %copy-start.4) | copy-done | bytes 280
  4.7 0.0 copy-start.5
  4.7 0.7 %copy-done.5 = f32[4,128]{1,0:T(4,128)S(1)} copy-done((f32[4,128]{1,0:T(4,128)S(1)}, f32[4,128]{1,0:T(4,128)}, u32[]{:S(2)}) %copy-start.5) | copy-done | bytes 2072
  5.4 0.0 copy-start.6
  5.4 0.7 %copy-done.6 = f32[8]{0:T(128)S(1)} copy-done((f32[8]{0:T(128)S(1)}, f32[8]{0:T(128)}, u32[]{:S(2)}) %copy-start.6) | copy-done | bytes 56
  6.1 49.8 %arnoldi.1 = (f32[6,5]{1,0:T(8,128)S(1)}, f32[6,64,4,128]{3,2,1,0:T(4,128)S(1)}) custom-call(f32[8,8]{1,0:T(8,128)S(1)} %copy-done.4, f32[8]{0:T(128)S(1)} %copy-done.6, f32[64,4,128]{2,1,0:T(4,128)S(1)} %copy-done, f32[64,4,128]{2,1,0:T(4,128)S(1)} %copy-done.1, f32[64,4,128]{2,1,0:T(4,128)S(1)} %copy-done.2, f32[4,128]{1,0:T(4,128)S(1)} %copy-done.5, ...), custom_call_target="tpu_custom_call" | custom-call | tf_op jit(solution)/shard_map/arnoldi/pallas_call | solution.py:311
  55.9 0.6 %copy.11 = f32[6,5]{1,0:T(8,128)} copy(f32[6,5]{1,0:T(8,128)S(1)} %get-tuple-element.4) | data formatting | bytes 240
  56.5 0.9 %copy.12 = f32[6,64,4,128]{3,2,1,0:T(4,128)} copy(f32[6,64,4,128]{3,2,1,0:T(4,128)S(1)} %get-tuple-element.5) | data formatting | bytes 1572864
Async XLA Ops:
  0.6 0.9 %copy-start = (f32[64,4,128]{2,1,0:T(4,128)S(1)}, f32[64,4,128]{2,1,0:T(4,128)}, u32[]{:S(2)}) copy-start(f32[64,4,128]{2,1,0:T(4,128)} %src_h.1) | copy-start | bytes 393220
  1.5 0.9 %copy-start.1 = (f32[64,4,128]{2,1,0:T(4,128)S(1)}, f32[64,4,128]{2,1,0:T(4,128)}, u32[]{:S(2)}) copy-start(f32[64,4,128]{2,1,0:T(4,128)} %x0_h.1) | copy-start | bytes 393220
  2.4 0.9 %copy-start.2 = (f32[64,4,128]{2,1,0:T(4,128)S(1)}, f32[64,4,128]{2,1,0:T(4,128)}, u32[]{:S(2)}) copy-start(f32[64,4,128]{2,1,0:T(4,128)} %rx_h.1) | copy-start | bytes 393220
  3.3 0.7 %copy-start.3 = (s32[4,4,128]{2,1,0:T(4,128)S(1)}, s32[4,4,128]{2,1,0:T(4,128)}, u32[]{:S(2)}) copy-start(s32[4,4,128]{2,1,0:T(4,128)} %wf_h.1) | copy-start | bytes 24580
  4.0 0.7 %copy-start.4 = (f32[8,8]{1,0:T(8,128)S(1)}, f32[8,8]{1,0:T(8,128)}, u32[]{:S(2)}) copy-start(f32[8,8]{1,0:T(8,128)} %line.1) | copy-start | bytes 772
  4.7 0.7 %copy-start.5 = (f32[4,128]{1,0:T(4,128)S(1)}, f32[4,128]{1,0:T(4,128)}, u32[]{:S(2)}) copy-start(f32[4,128]{1,0:T(4,128)} %st_h.1) | copy-start | bytes 6148
  5.4 0.7 %copy-start.6 = (f32[8]{0:T(128)S(1)}, f32[8]{0:T(128)}, u32[]{:S(2)}) copy-start(f32[8]{0:T(128)} %fd.1) | copy-start | bytes 100

commit v2 on v1

--- a/solution.py
+++ b/solution.py
@@ -73,34 +73,32 @@
     return a
 
 
-def kernel(sizes, line, fd, src_h, x0_h, rx_h, st_h, wf_h, hess, out_h,
-           srcv, xin, rxin, stin, wfin, w, rx, st, op, qf, sxy, rxy, row1, buf1, row2, buf2, vout,
-           lsem, osem, hs, hr, s1, r1, s2, r2):
+def kernel(sizes, line, fd, src_h, x0_h, rx_h, st_h, wf_h, hess, vout,
+           xl, sl, rl, stl, wfl, opl, w, sv, rx, st, op, gw, pk, lb, rb, qs, qr, gqs, gql, gqr, qf,
+           row1, buf1, row2, buf2,
+           lsem, hs, hr, s1, r1, s2, r2):
     ny, nc, nx, nz = sizes
     y, c, x, z = (lax.axis_index(a) for a in AXES)
 
-    def gx(s):
-        g = lax.rem(y * nc + c + ny * nc + s, ny * nc)
-        return (g // nc, lax.rem(g, nc), x, z)
-
-    def gy(s):
-        g = lax.rem(x * nz + z + nx * nz + s, nx * nz)
-        return (y, c, g // nz, lax.rem(g, nz))
-
-    east, west, north, south = gx(1), gx(-1), gy(1), gy(-1)
+    def at(dx, dy):
+        i = lax.rem(y * nc + c + ny * nc + dx, ny * nc)
+        j = lax.rem(x * nz + z + nx * nz + dy, nx * nz)
+        return (i // nc, lax.rem(i, nc), j // nz, lax.rem(j, nz))
+
     group1 = [
         (lax.rem(y + i, ny), lax.rem(c + j, nc), lax.rem(x + k, nx), z)
         for i in range(ny) for j in range(nc) for k in range(nx) if i + j + k > 0
     ]
     group2 = [(y, c, x, lax.rem(z + k, nz)) for k in range(1, nz)]
+    around = {(i, j): at(i, j) for i in (-1, 0, 1) for j in (-1, 0, 1) if (i, j) != (0, 0)}
     barrier = pltpu.get_barrier_semaphore()
-    greeted = [east, west, north, south] + group1 + group2
+    greeted = list(around.values()) + group1 + group2
     for peer in greeted:
         pl.semaphore_signal(barrier, inc=1, device_id=peer, device_id_type=MESH)
-    loads = [
-        pltpu.make_async_copy(a, b, lsem.at[i])
-        for i, (a, b) in enumerate([(x0_h, xin), (rx_h, rxin), (src_h, srcv), (st_h, stin), (wf_h, wfin)])
-    ]
+    own = pl.ds(0, 4)
+    pairs = [(x0_h, xl.at[:, own, :]), (rx_h, rl.at[:, own, :]), (src_h, sl.at[:, own, :]), (st_h, stl.at[own, :]),
+             (wf_h, wfl.at[:, own, :]), (x0_h, w.at[0, :, own, :]), (rx_h, rx.at[:, own, :]), (src_h, sv.at[:, own, :])]
+    loads = [pltpu.make_async_copy(a, b, lsem.at[i]) for i, (a, b) in enumerate(pairs)]
     for cp in loads:
         cp.start()
 
@@ -116,79 +114,208 @@
     lane = lax.broadcasted_iota(jnp.int32, (8, 128), 1)
     sub = lax.broadcasted_iota(jnp.int32, (8, 128), 0)
     group = lane // 16
-    zero4 = jnp.zeros((4, 128), jnp.float32)
-    for cp in loads:
-        cp.wait()
-    for q in range(n * n):
-        w[0, q, 0:4, :] = xin[q]
-        w[0, q, 4:8, :] = zero4
-        rx[q, 0:4, :] = rxin[q] - shift
-        rx[q, 4:8, :] = zero4
-    st[0:4, :] = stin[...]
-    st[4:8, :] = zero4
-    for f in range(4):
-        op[f, 0:4, :] = 1.0 - wfin[f].astype(jnp.float32)
-        op[f, 4:8, :] = zero4
+    slot16 = lax.rem(lane, 16)
+
+    def lroll(t, s):
+        s = s % 128
+        return t if s == 0 else pltpu.roll(t, s, 1)
+
+    def gather_groups(items, s):
+        out = lroll(items[0], s)
+        for a in range(1, len(items)):
+            out = jnp.where(group == a, lroll(items[a], 16 * a + s), out)
+        return out
+
+    cline, cface = [], []
+    for k in range(n):
+        t = jnp.zeros((8, 128), jnp.float32)
+        for a in range(n):
+            t = jnp.where(group == a, lop[a][(a - k) % n], t)
+        cline.append(t)
+        cface.append(jnp.where(group == 0, g[(n - k) % n], jnp.where(group == n - 1, g[k], 0.0)))
+
+    def x_faces(v):
+        qw = [tree([g[i] * v(i, b) for i in range(n)], jnp.add) for b in range(n)]
+        qe = [tree([g[i] * v(n - 1 - i, b) for i in range(n)], jnp.add) for b in range(n)]
+        return qw, qe
+
+    def strip_faces(t):
+        rolled = [t] + [lroll(t, 16 * k) for k in range(1, n)]
+        return rolled, tree([cface[k] * rolled[k] for k in range(n)], jnp.add)
+
+    for cp in loads[:5]:
+        cp.wait()
+    opl[...] = 1.0 - wfl[...].astype(jnp.float32)
+    qw, qe = x_faces(lambda a, b: xl[a * n + b])
+    for b in range(n):
+        qs[0, 0, pl.ds(b, 1), :] = qw[b][2:3, :]
+        qs[0, 1, pl.ds(b, 1), :] = qe[b][1:2, :]
+    for b in range(n):
+        px = gather_groups([xl[a * n + b] for a in range(n)], 6)
+        ps = gather_groups([sl[a * n + b] for a in range(n)], 6)
+        pr = gather_groups([rl[a * n + b] for a in range(n)], 6)
+        pk[0, b] = jnp.where(slot16 < 6, px, jnp.where(slot16 < 11, lroll(ps, 5), lroll(pr, 10)))
+        pk[1, b] = jnp.where(slot16 < 6, lroll(px, -6), jnp.where(slot16 < 11, ps, lroll(pr, 5)))
+        face = strip_faces(px)[1]
+        gqs[0, 0, pl.ds(b, 1), :] = face[2:3, :]
+        gqs[0, 1, pl.ds(b, 1), :] = face[1:2, :]
+    pst = gather_groups([stl[...]] + [opl[f] for f in range(4)], 6)
+    pk[0, n] = pst
+    pk[1, n] = pst
     pl.semaphore_wait(barrier, len(greeted))
 
-    def apply(k):
-        def v(a, b):
-            return w[k, a * n + b]
-
-        pn = ps = jnp.zeros((8, 128), jnp.float32)
-        for a in range(n):
-            qs = tree([g[i] * v(a, i) for i in range(n)], jnp.add)
-            qn = tree([g[i] * v(a, n - 1 - i) for i in range(n)], jnp.add)
-            qf[2, a] = qs
-            qf[3, a] = qn
-            pn = jnp.where(group == a, pltpu.roll(qn, (16 * a + 1) % 128, 1), pn)
-            ps = jnp.where(group == a, pltpu.roll(qs, 16 * a, 1), ps)
-        sxy[k, 2] = ps
-        sxy[k, 3] = pn
-        for b in range(n):
-            qw = tree([g[i] * v(i, b) for i in range(n)], jnp.add)
-            qe = tree([g[i] * v(n - 1 - i, b) for i in range(n)], jnp.add)
-            qf[0, b] = qw
-            qf[1, b] = qe
-            sxy[k, 0, pl.ds(b, 1), :] = qw[0:1, :]
-            sxy[k, 1, pl.ds(b, 1), :] = qe[3:4, :]
-        copies = []
-        for f, peer in ((3, north), (2, south), (1, east), (0, west)):
+    def send(copies, peer, pieces, first):
+        for i, (a, b) in enumerate(pieces):
             cp = pltpu.make_async_remote_copy(
-                src_ref=sxy.at[k, f], dst_ref=rxy.at[k, f], send_sem=hs.at[k, f], recv_sem=hr.at[k, f],
+                src_ref=a, dst_ref=b, send_sem=hs.at[first + i], recv_sem=hr.at[first + i],
                 device_id=peer, device_id_type=MESH)
             cp.start()
             copies.append(cp)
+        return first + len(pieces)
+
+    def rows(lo):
+        return pl.ds(lo, 2)
+
+    copies, used = [], 0
+    for dy, k, dst in ((1, 0, lb), (-1, 1, rb)):
+        used = send(copies, around[0, dy], [(pk.at[k, :, own, :], dst.at[:, own, :])], used)
+    for dy, k, dst, gq in ((1, 0, lb, gql), (-1, 1, rb, gqr)):
+        for dx, lo, to in ((1, 2, 6), (-1, 0, 4)):
+            side = 1 if dx > 0 else 0
+            used = send(copies, around[dx, dy], [
+                (pk.at[k, :, rows(lo), :], dst.at[:, rows(to), :]), (gqs.at[0, side], gq.at[0, side])], used)
+    for dx, lo, to in ((1, 2, 6), (-1, 0, 4)):
+        side = 1 if dx > 0 else 0
+        used = send(copies, around[dx, 0], [
+            (xl.at[:, rows(lo), :], w.at[0, :, rows(to), :]),
+            (rl.at[:, rows(lo), :], rx.at[:, rows(to), :]),
+            (sl.at[:, rows(lo), :], sv.at[:, rows(to), :]),
+            (stl.at[rows(lo), :], st.at[rows(to), :]),
+            (opl.at[:, rows(lo), :], op.at[:, rows(to), :]),
+            (qs.at[0, side], qr.at[0, side])], used)
+    st[0:4, :] = stl[0:4, :]
+    op[:, 0:4, :] = opl[:, 0:4, :]
+    for cp in loads[5:]:
+        cp.wait()
+    for cp in copies:
+        cp.wait()
+
+    before_half = slot16 < 6
+    gsv, grx = [], []
+    for b in range(n):
+        lo, hi = lb[b], rb[b]
+        gw[0, b] = jnp.where(before_half, lo, lroll(hi, 6))
+        gsv.append(jnp.where(before_half, lroll(lo, -5), hi))
+        grx.append(jnp.where(before_half, lroll(lo, -10), lroll(hi, -5)))
+    both = jnp.where(before_half, lb[n], rb[n])
+    spreads = []
+    for f in range(5):
+        t = jnp.where(group == f, both, 0.0)
+        for s in (16, 32, 64):
+            t = t + lroll(t, s)
+        spreads.append(t)
+    gst = spreads[0]
+    gopw = jnp.where(group == 0, spreads[1], 0.0)
+    gope = jnp.where(group == n - 1, spreads[2], 0.0)
+    gops, gopn = spreads[3], spreads[4]
+    for side in (0, 1):
+        gqr[0, side] = jnp.where(before_half, gql[0, side], gqr[0, side])
+
+    def apply(k, last=False, fresh=None):
+        wide = k != 2
+
+        def v(a, b):
+            return w[k, a * n + b]
+
+        def keep(a, b, t):
+            if wide:
+                w[k + 1, a * n + b] = t
+            else:
+                w[k + 1, a * n + b, 0:4, :] = t[0:4, :]
+
+        gv = [gw[k, b] for b in range(n)]
+        gqsouth = tree([g[i] * gv[i] for i in range(n)], jnp.add)
+        gqnorth = tree([g[i] * gv[n - 1 - i] for i in range(n)], jnp.add)
+        qsouth = [tree([g[i] * v(a, i) for i in range(n)], jnp.add) for a in range(n)]
+        qnorth = [tree([g[i] * v(a, n - 1 - i) for i in range(n)], jnp.add) for a in range(n)]
+        for a in range(n):
+            below = jnp.where(lane == 0, lroll(gqnorth, -(16 * a + 5)), lroll(qnorth[a], 1))
+            above = jnp.where(lane == 127, lroll(gqsouth, 121 - 16 * a), lroll(qsouth[a], -1))
+            qf[2, a] = qsouth[a] - op[2] * below
+            qf[3, a] = qnorth[a] - op[3] * above
+        if not last:
+            mn = gather_groups(qnorth, 7)
+            ms = gather_groups(qsouth, 5)
+            sterm = gqsouth - gops * jnp.where(slot16 == 6, mn, lroll(gqnorth, 1))
+            nterm = gqnorth - gopn * jnp.where(slot16 == 5, ms, lroll(gqsouth, -1))
+            for b in range(n):
+                rolled, face = strip_faces(gv[b])
+                prev = pltpu.roll(lroll(face, 16), 1, 0)
+                nxt = pltpu.roll(lroll(face, -16), 7, 0)
+                if fresh is not None:
+                    prev = jnp.where(sub == 6, jnp.broadcast_to(lroll(gqr[fresh, 1, pl.ds(b, 1), :], 16), (8, 128)), prev)
+                    nxt = jnp.where(sub == 5, jnp.broadcast_to(lroll(gqr[fresh, 0, pl.ds(b, 1), :], -16), (8, 128)), nxt)
+                acc = tree([cline[i] * rolled[i] for i in range(n)] + [lop[b][i] * gv[i] for i in range(n)], jnp.add)
+                t = grx[b] * gv[b] + gst * acc + (face - (gopw * prev + gope * nxt))
+                if b == 0:
+                    t = t + sterm
+                if b == n - 1:
+                    t = t + nterm
+                t = t - (gsv[b] if k == 0 else shift * gv[b])
+                if wide:
+                    gw[k + 1, b] = t
+                else:
+                    gw[k + 1, b, 0:4, :] = t[0:4, :]
         stiff = st[...]
         for b in range(n):
             col = [v(i, b) for i in range(n)]
+            qwest = tree([g[i] * col[i] for i in range(n)], jnp.add)
+            qeast = tree([g[i] * col[n - 1 - i] for i in range(n)], jnp.add)
+            prev = pltpu.roll(qeast, 1, 0)
+            nxt = pltpu.roll(qwest, 7, 0)
+            if fresh is not None:
+                prev = jnp.where(sub == 6, jnp.broadcast_to(qr[fresh, 1, pl.ds(b, 1), :], (8, 128)), prev)
+                nxt = jnp.where(sub == 5, jnp.broadcast_to(qr[fresh, 0, pl.ds(b, 1), :], (8, 128)), nxt)
             for a in range(n):
                 acc = tree([lop[a][i] * col[i] for i in range(n)] + [lop[b][i] * v(a, i) for i in range(n)], jnp.add)
-                w[k + 1, a * n + b] = rx[a * n + b] * col[a] + stiff * acc
-        for cp in copies:
-            cp.wait()
-        for b in range(n):
-            before = jnp.where(sub == 0, jnp.broadcast_to(rxy[k, 1, pl.ds(b, 1), :], (8, 128)), pltpu.roll(qf[1, b], 1, 0))
-            after = jnp.where(sub == 3, jnp.broadcast_to(rxy[k, 0, pl.ds(b, 1), :], (8, 128)), pltpu.roll(qf[0, b], 7, 0))
-            w[k + 1, b] = w[k + 1, b] + (qf[0, b] - op[0] * before)
-            w[k + 1, 7 * n + b] = w[k + 1, 7 * n + b] + (qf[1, b] - op[1] * after)
-        rn = rxy[k, 3]
-        rs = rxy[k, 2]
-        for a in range(n):
-            before = jnp.where(lane == 0, pltpu.roll(rn, (128 - 16 * a) % 128, 1), pltpu.roll(qf[3, a], 1, 1))
-            after = jnp.where(lane == 127, pltpu.roll(rs, (127 - 16 * a) % 128, 1), pltpu.roll(qf[2, a], 127, 1))
-            w[k + 1, a * n] = w[k + 1, a * n] + (qf[2, a] - op[2] * before)
-            w[k + 1, a * n + 7] = w[k + 1, a * n + 7] + (qf[3, a] - op[3] * after)
-
-    apply(0)
-    for q in range(n * n):
-        w[1, q, 0:4, :] = w[1, q, 0:4, :] - (srcv[q] - shift * xin[q])
-
-    def step(k, carry):
-        apply(k)
-        return carry
-
-    lax.fori_loop(1, NV, step, 0)
+                if k == 0:
+                    t = rx[a * n + b] * col[a] - sv[a * n + b] + stiff * acc
+                else:
+                    t = (rx[a * n + b] - shift) * col[a] + stiff * acc
+                if a == 0:
+                    t = t + (qwest - op[0] * prev)
+                if a == n - 1:
+                    t = t + (qeast - op[1] * nxt)
+                if b == 0:
+                    t = t + qf[2, a]
+                if b == n - 1:
+                    t = t + qf[3, a]
+                keep(a, b, t)
+
+    apply(0, fresh=0)
+    apply(1)
+    apply(2)
+    qw, qe = x_faces(lambda a, b: w[3, a * n + b, 0:4, :])
+    for b in range(n):
+        qs[1, 0, pl.ds(b, 1), :] = qw[b][2:3, :]
+        qs[1, 1, pl.ds(b, 1), :] = qe[b][1:2, :]
+        t = jnp.concatenate([gw[3, b, 0:4, :]] * 2, axis=0)
+        face = strip_faces(t)[1]
+        gqs[1, 0, pl.ds(b, 1), :] = face[2:3, :]
+        gqs[1, 1, pl.ds(b, 1), :] = face[1:2, :]
+    copies = []
+    for dx, lo, to in ((1, 2, 6), (-1, 0, 4)):
+        side = 1 if dx > 0 else 0
+        used = send(copies, around[dx, 0], [
+            (w.at[3, :, rows(lo), :], w.at[3, :, rows(to), :]),
+            (gw.at[3, :, rows(lo), :], gw.at[3, :, rows(to), :]),
+            (qs.at[1, side], qr.at[1, side]),
+            (gqs.at[1, side], gqr.at[1, side])], used)
+    for cp in copies:
+        cp.wait()
+    apply(3, fresh=1)
+    apply(4)
+    apply(5, last=True)
 
     def gram(q, acc):
         vals = [w[i + 1, q] for i in range(NV)]
@@ -279,7 +406,6 @@
 
     weights = [[jnp.broadcast_to(coefs[j][0][i:i + 1, :], (8, 128)) for i in range(j + 1)] for j in range(NV)]
 
-    outs = []
     for j in range(NV):
         def combine(q, carry, j=j):
             t = tree([weights[j][i] * w[i + 1, q] for i in range(j + 1)], jnp.add)
@@ -287,11 +413,6 @@
             return carry
 
         lax.fori_loop(0, n * n, combine, 0, unroll=8)
-        cp = pltpu.make_async_copy(vout.at[j], out_h.at[j], osem.at[j])
-        cp.start()
-        outs.append(cp)
-    for cp in outs:
-        cp.wait()
 
 
 def solution(mesh):
@@ -304,27 +425,31 @@
     def body(source, initial, reaction, stiffness, line_op, face_deriv, wall_flags):
         nodes, ex, ey = source.shape
         n1, n2 = ny * nc * nx - 1, nz - 1
-        anywhere = pl.BlockSpec(memory_space=pl.ANY)
+        hbm = pl.BlockSpec(memory_space=pltpu.HBM)
         scalars = pl.BlockSpec(memory_space=pltpu.SMEM)
+        local = pl.BlockSpec(memory_space=pltpu.VMEM)
         vm = pltpu.VMEM
         dma = pltpu.SemaphoreType.DMA
+        tile = (8, ey)
+        sends = 2 + 8 + 12 + 8
         return pl.pallas_call(
             functools.partial(kernel, sizes),
             out_shape=(
                 jax.ShapeDtypeStruct((NV, ITERS), f32),
                 jax.ShapeDtypeStruct((NV, nodes, ex, ey), f32),
             ),
-            in_specs=[scalars, scalars] + [anywhere] * 5,
-            out_specs=(pl.BlockSpec(memory_space=pltpu.VMEM), anywhere),
+            in_specs=[scalars, scalars] + [hbm] * 5,
+            out_specs=(local, local),
             scratch_shapes=[
-                vm((nodes, ex, ey), f32), vm((nodes, ex, ey), f32), vm((nodes, ex, ey), f32),
-                vm((ex, ey), f32), vm((4, ex, ey), jnp.int32),
-                vm((NV + 1, nodes, 8, ey), f32), vm((nodes, 8, ey), f32), vm((8, ey), f32), vm((4, 8, ey), f32),
-                vm((4, 8, 8, ey), f32),
-                vm((NV, 4, 8, ey), f32), vm((NV, 4, 8, ey), f32),
+                vm((nodes,) + tile, f32), vm((nodes,) + tile, f32), vm((nodes,) + tile, f32), vm(tile, f32),
+                vm((4,) + tile, jnp.int32), vm((4,) + tile, f32),
+                vm((NV + 1, nodes) + tile, f32), vm((nodes,) + tile, f32), vm((nodes,) + tile, f32), vm(tile, f32),
+                vm((4,) + tile, f32), vm((NV, 8) + tile, f32),
+                vm((2, 9) + tile, f32), vm((9,) + tile, f32), vm((9,) + tile, f32),
+                vm((2, 2) + tile, f32), vm((2, 2) + tile, f32), vm((2, 2) + tile, f32), vm((1, 2) + tile, f32),
+                vm((2, 2) + tile, f32), vm((4, 8) + tile, f32),
                 vm((1, 128), f32), vm((n1, 1, 128), f32), vm((2, 128), f32), vm((n2, 2, 128), f32),
-                vm((NV, nodes, ex, ey), f32),
-                dma((5,)), dma((NV,)), dma((NV, 4)), dma((NV, 4)), dma((n1,)), dma((n1,)), dma((n2,)), dma((n2,)),
+                dma((8,)), dma((sends,)), dma((sends,)), dma((n1,)), dma((n1,)), dma((n2,)), dma((n2,)),
             ],
             compiler_params=pltpu.CompilerParams(
                 collective_id=0, has_side_effects=True, vmem_limit_bytes=48 * 1024 * 1024),

time: 57.6 us -> 41.9 us (0.73)
  Pallas kernels: 49.8 us -> 34.1 us
    pallas_call x1, Pallas kernels: 49.8 us -> 34.1 us  [body(): pl.pallas_call(functools.partial(kernel, sizes), out_shape=(jax.ShapeDtyp...]
where the time goes in v2:
time: 41.9 us; the launch traced here: 41.7 us
  Pallas kernels  34.1 us (81%)
  local copies, waits for them, and re-layouts  6.9 us (16%)
  between operations  0.66 us (2%)
    pallas_call x1, Pallas kernels, body(): pl.pallas_call(functools.partial(kernel, sizes), out_shape=(jax.ShapeDtyp...  34.1 us
    unnamed x16, local copies, waits for them, and re-layouts  6.9 us

profile of v2, /device:TPU:1, one launch (start us, length us, event | category | flops | bytes accessed | tf_op | source)
XLA Modules:
  0.0 41.7 jit_solution(8566644122501994550)
XLA Ops:
  0.6 0.0 copy-start
  0.6 0.9 %copy-done = f32[64,4,128]{2,1,0:T(4,128)S(1)} copy-done((f32[64,4,128]{2,1,0:T(4,128)S(1)}, f32[64,4,128]{2,1,0:T(4,128)}, u32[]{:S(2)}) %copy-start) | copy-done | bytes 131096
  1.5 0.0 copy-start.1
  1.5 0.9 %copy-done.1 = f32[64,4,128]{2,1,0:T(4,128)S(1)} copy-done((f32[64,4,128]{2,1,0:T(4,128)S(1)}, f32[64,4,128]{2,1,0:T(4,128)}, u32[]{:S(2)}) %copy-start.1) | copy-done | bytes 131096
  2.4 0.0 copy-start.2
  2.4 0.9 %copy-done.2 = f32[64,4,128]{2,1,0:T(4,128)S(1)} copy-done((f32[64,4,128]{2,1,0:T(4,128)S(1)}, f32[64,4,128]{2,1,0:T(4,128)}, u32[]{:S(2)}) %copy-start.2) | copy-done | bytes 131096
  3.3 0.0 copy-start.3
  3.3 0.7 %copy-done.3 = s32[4,4,128]{2,1,0:T(4,128)S(1)} copy-done((s32[4,4,128]{2,1,0:T(4,128)S(1)}, s32[4,4,128]{2,1,0:T(4,128)}, u32[]{:S(2)}) %copy-start.3) | copy-done | bytes 8216
  4.0 0.0 copy-start.4
  4.0 0.7 %copy-done.4 = f32[8,8]{1,0:T(8,128)S(1)} copy-done((f32[8,8]{1,0:T(8,128)S(1)}, f32[8,8]{1,0:T(8,128)}, u32[]{:S(2)}) %copy-start.4) | copy-done | bytes 280
  4.7 0.0 copy-start.5
  4.7 0.7 %copy-done.5 = f32[4,128]{1,0:T(4,128)S(1)} copy-done((f32[4,128]{1,0:T(4,128)S(1)}, f32[4,128]{1,0:T(4,128)}, u32[]{:S(2)}) %copy-start.5) | copy-done | bytes 2072
  5.4 0.0 copy-start.6
  5.4 0.7 %copy-done.6 = f32[8]{0:T(128)S(1)} copy-done((f32[8]{0:T(128)S(1)}, f32[8]{0:T(128)}, u32[]{:S(2)}) %copy-start.6) | copy-done | bytes 56
  6.1 34.1 %arnoldi.1 = (f32[6,5]{1,0:T(8,128)S(1)}, f32[6,64,4,128]{3,2,1,0:T(4,128)S(1)}) custom-call(f32[8,8]{1,0:T(8,128)S(1)} %copy-done.4, f32[8]{0:T(128)S(1)} %copy-done.6, f32[64,4,128]{2,1,0:T(4,128)S(1)} %copy-done, f32[64,4,128]{2,1,0:T(4,128)S(1)} %copy-done.1, f32[64,4,128]{2,1,0:T(4,128)S(1)} %copy-done.2, f32[4,128]{1,0:T(4,128)S(1)} %copy-done.5, ...), custom_call_target="tpu_custom_call" | custom-call | tf_op jit(solution)/shard_map/arnoldi/pallas_call | solution.py:435
  40.2 0.6 %copy.11 = f32[6,5]{1,0:T(8,128)} copy(f32[6,5]{1,0:T(8,128)S(1)} %get-tuple-element.4) | data formatting | bytes 240
  40.8 0.9 %copy.12 = f32[6,64,4,128]{3,2,1,0:T(4,128)} copy(f32[6,64,4,128]{3,2,1,0:T(4,128)S(1)} %get-tuple-element.5) | data formatting | bytes 1572864
Async XLA Ops:
  0.6 0.9 %copy-start = (f32[64,4,128]{2,1,0:T(4,128)S(1)}, f32[64,4,128]{2,1,0:T(4,128)}, u32[]{:S(2)}) copy-start(f32[64,4,128]{2,1,0:T(4,128)} %src_h.1) | copy-start | bytes 393220
  1.5 0.9 %copy-start.1 = (f32[64,4,128]{2,1,0:T(4,128)S(1)}, f32[64,4,128]{2,1,0:T(4,128)}, u32[]{:S(2)}) copy-start(f32[64,4,128]{2,1,0:T(4,128)} %x0_h.1) | copy-start | bytes 393220
  2.4 0.9 %copy-start.2 = (f32[64,4,128]{2,1,0:T(4,128)S(1)}, f32[64,4,128]{2,1,0:T(4,128)}, u32[]{:S(2)}) copy-start(f32[64,4,128]{2,1,0:T(4,128)} %rx_h.1) | copy-start | bytes 393220
  3.3 0.7 %copy-start.3 = (s32[4,4,128]{2,1,0:T(4,128)S(1)}, s32[4,4,128]{2,1,0:T(4,128)}, u32[]{:S(2)}) copy-start(s32[4,4,128]{2,1,0:T(4,128)} %wf_h.1) | copy-start | bytes 24580
  4.0 0.7 %copy-start.4 = (f32[8,8]{1,0:T(8,128)S(1)}, f32[8,8]{1,0:T(8,128)}, u32[]{:S(2)}) copy-start(f32[8,8]{1,0:T(8,128)} %line.1) | copy-start | bytes 772
  4.7 0.7 %copy-start.5 = (f32[4,128]{1,0:T(4,128)S(1)}, f32[4,128]{1,0:T(4,128)}, u32[]{:S(2)}) copy-start(f32[4,128]{1,0:T(4,128)} %st_h.1) | copy-start | bytes 6148
  5.4 0.7 %copy-start.6 = (f32[8]{0:T(128)S(1)}, f32[8]{0:T(128)}, u32[]{:S(2)}) copy-start(f32[8]{0:T(128)} %fd.1) | copy-start | bytes 100

commit v3 on v2

--- a/solution.py
+++ b/solution.py
@@ -73,9 +73,9 @@
     return a
 
 
-def kernel(sizes, line, fd, src_h, x0_h, rx_h, st_h, wf_h, hess, vout,
-           xl, sl, rl, stl, wfl, opl, w, sv, rx, st, op, gw, pk, lb, rb, qs, qr, gqs, gql, gqr, qf,
-           row1, buf1, row2, buf2,
+def kernel(sizes, line_h, fd_h, src_h, x0_h, rx_h, st_h, wf_h, w, cw, hm,
+           xl, sl, rl, stl, wfl, opl, x0, sv, rx, st, op, gw, pk, lb, rb, qs, qr, gqs, gql, gqr, qf,
+           row1, buf1, row2, buf2, line, fd,
            lsem, hs, hr, s1, r1, s2, r2):
     ny, nc, nx, nz = sizes
     y, c, x, z = (lax.axis_index(a) for a in AXES)
@@ -91,17 +91,19 @@
     ]
     group2 = [(y, c, x, lax.rem(z + k, nz)) for k in range(1, nz)]
     around = {(i, j): at(i, j) for i in (-1, 0, 1) for j in (-1, 0, 1) if (i, j) != (0, 0)}
+    own = pl.ds(0, 4)
+    pairs = [(line_h, line), (fd_h, fd), (x0_h, xl.at[:, own, :]), (rx_h, rl.at[:, own, :]), (src_h, sl.at[:, own, :]), (st_h, stl.at[own, :]),
+             (wf_h, wfl.at[:, own, :]), (x0_h, x0.at[:, own, :]), (rx_h, rx.at[:, own, :]), (src_h, sv.at[:, own, :])]
+    loads = [pltpu.make_async_copy(a, b, lsem.at[i]) for i, (a, b) in enumerate(pairs)]
+    for cp in loads:
+        cp.start()
+
     barrier = pltpu.get_barrier_semaphore()
     greeted = list(around.values()) + group1 + group2
     for peer in greeted:
         pl.semaphore_signal(barrier, inc=1, device_id=peer, device_id_type=MESH)
-    own = pl.ds(0, 4)
-    pairs = [(x0_h, xl.at[:, own, :]), (rx_h, rl.at[:, own, :]), (src_h, sl.at[:, own, :]), (st_h, stl.at[own, :]),
-             (wf_h, wfl.at[:, own, :]), (x0_h, w.at[0, :, own, :]), (rx_h, rx.at[:, own, :]), (src_h, sv.at[:, own, :])]
-    loads = [pltpu.make_async_copy(a, b, lsem.at[i]) for i, (a, b) in enumerate(pairs)]
-    for cp in loads:
-        cp.start()
-
+    for cp in loads[:2]:
+        cp.wait()
     n = P_SIZE
     total = float(ny * nc * nx * nz * src_h.shape[0] * src_h.shape[1] * src_h.shape[2])
     lop = [[line[i, j] for j in range(n)] for i in range(n)]
@@ -143,7 +145,7 @@
         rolled = [t] + [lroll(t, 16 * k) for k in range(1, n)]
         return rolled, tree([cface[k] * rolled[k] for k in range(n)], jnp.add)
 
-    for cp in loads[:5]:
+    for cp in loads[2:7]:
         cp.wait()
     opl[...] = 1.0 - wfl[...].astype(jnp.float32)
     qw, qe = x_faces(lambda a, b: xl[a * n + b])
@@ -156,9 +158,8 @@
         pr = gather_groups([rl[a * n + b] for a in range(n)], 6)
         pk[0, b] = jnp.where(slot16 < 6, px, jnp.where(slot16 < 11, lroll(ps, 5), lroll(pr, 10)))
         pk[1, b] = jnp.where(slot16 < 6, lroll(px, -6), jnp.where(slot16 < 11, ps, lroll(pr, 5)))
-        face = strip_faces(px)[1]
-        gqs[0, 0, pl.ds(b, 1), :] = face[2:3, :]
-        gqs[0, 1, pl.ds(b, 1), :] = face[1:2, :]
+    gqs[0, 0] = lroll(qs[0, 0], 6)
+    gqs[0, 1] = lroll(qs[0, 1], 118)
     pst = gather_groups([stl[...]] + [opl[f] for f in range(4)], 6)
     pk[0, n] = pst
     pk[1, n] = pst
@@ -187,7 +188,7 @@
     for dx, lo, to in ((1, 2, 6), (-1, 0, 4)):
         side = 1 if dx > 0 else 0
         used = send(copies, around[dx, 0], [
-            (xl.at[:, rows(lo), :], w.at[0, :, rows(to), :]),
+            (xl.at[:, rows(lo), :], x0.at[:, rows(to), :]),
             (rl.at[:, rows(lo), :], rx.at[:, rows(to), :]),
             (sl.at[:, rows(lo), :], sv.at[:, rows(to), :]),
             (stl.at[rows(lo), :], st.at[rows(to), :]),
@@ -195,7 +196,7 @@
             (qs.at[0, side], qr.at[0, side])], used)
     st[0:4, :] = stl[0:4, :]
     op[:, 0:4, :] = opl[:, 0:4, :]
-    for cp in loads[5:]:
+    for cp in loads[7:]:
         cp.wait()
     for cp in copies:
         cp.wait()
@@ -225,13 +226,13 @@
         wide = k != 2
 
         def v(a, b):
-            return w[k, a * n + b]
+            return w[k - 1, a * n + b] if k else x0[a * n + b]
 
         def keep(a, b, t):
             if wide:
-                w[k + 1, a * n + b] = t
+                w[k, a * n + b] = t
             else:
-                w[k + 1, a * n + b, 0:4, :] = t[0:4, :]
+                w[k, a * n + b, 0:4, :] = t[0:4, :]
 
         gv = [gw[k, b] for b in range(n)]
         gqsouth = tree([g[i] * gv[i] for i in range(n)], jnp.add)
@@ -295,7 +296,7 @@
     apply(0, fresh=0)
     apply(1)
     apply(2)
-    qw, qe = x_faces(lambda a, b: w[3, a * n + b, 0:4, :])
+    qw, qe = x_faces(lambda a, b: w[2, a * n + b, 0:4, :])
     for b in range(n):
         qs[1, 0, pl.ds(b, 1), :] = qw[b][2:3, :]
         qs[1, 1, pl.ds(b, 1), :] = qe[b][1:2, :]
@@ -307,21 +308,28 @@
     for dx, lo, to in ((1, 2, 6), (-1, 0, 4)):
         side = 1 if dx > 0 else 0
         used = send(copies, around[dx, 0], [
-            (w.at[3, :, rows(lo), :], w.at[3, :, rows(to), :]),
+            (w.at[2, :, rows(lo), :], w.at[2, :, rows(to), :]),
             (gw.at[3, :, rows(lo), :], gw.at[3, :, rows(to), :]),
             (qs.at[1, side], qr.at[1, side]),
             (gqs.at[1, side], gqr.at[1, side])], used)
+    def gram(pairs):
+        top = max(j for i, j in pairs) + 1
+
+        def body(q, acc):
+            vals = [w[i, q] for i in range(top)]
+            return tuple(t + vals[i] * vals[j] for t, (i, j) in zip(acc, pairs))
+
+        return lax.fori_loop(0, n * n, body, tuple(jnp.zeros((8, 128), jnp.float32) for _ in pairs), unroll=2)
+
+    early = [p for p in PAIRS if p[1] < 2]
+    first = gram(early)
     for cp in copies:
         cp.wait()
     apply(3, fresh=1)
     apply(4)
     apply(5, last=True)
 
-    def gram(q, acc):
-        vals = [w[i + 1, q] for i in range(NV)]
-        return tuple(t + vals[i] * vals[j] for t, (i, j) in zip(acc, PAIRS))
-
-    acc = lax.fori_loop(0, n * n, gram, tuple(jnp.zeros((8, 128), jnp.float32) for _ in PAIRS))
+    acc = first + gram(PAIRS[len(early):])
     line_row = jnp.zeros((8, 128), jnp.float32)
     for base in range(0, len(PAIRS), 8):
         packed = jnp.zeros((8, 128), jnp.float32)
@@ -402,17 +410,30 @@
             hmat = jnp.where((sub == i) & (lane == j), hs_j[i], hmat)
         u = tree([u] + [mul1(coefs[i], -hs_j[i]) for i in range(j + 1)], add2)
         e = tree([e] + [mul1(images[i], -hs_j[i]) for i in range(j + 1)], add2)
-    hess[...] = hmat[0:NV, 0:ITERS]
-
-    weights = [[jnp.broadcast_to(coefs[j][0][i:i + 1, :], (8, 128)) for i in range(j + 1)] for j in range(NV)]
-
+    hm[...] = hmat
     for j in range(NV):
-        def combine(q, carry, j=j):
-            t = tree([weights[j][i] * w[i + 1, q] for i in range(j + 1)], jnp.add)
+        cw[j] = coefs[j][0]
+
+
+def output_kernel(w, cw, hm, hess_h, out_h, hess, vout, sem):
+    nodes = w.shape[1]
+    hess[...] = hm[0:NV, 0:ITERS]
+    outs = [pltpu.make_async_copy(hess, hess_h, sem.at[0])]
+    outs[0].start()
+    for j in range(NV):
+        weights = [jnp.broadcast_to(cw[j, pl.ds(i, 1), :], (8, 128)) for i in range(j + 1)]
+
+        def combine(q, carry):
+            t = tree([weights[i] * w[i, q] for i in range(j + 1)], jnp.add)
             vout[j, q] = t[0:4, :]
             return carry
 
-        lax.fori_loop(0, n * n, combine, 0, unroll=8)
+        lax.fori_loop(0, nodes, combine, 0, unroll=8)
+        cp = pltpu.make_async_copy(vout.at[j], out_h.at[j], sem.at[j + 1])
+        cp.start()
+        outs.append(cp)
+    for cp in outs:
+        cp.wait()
 
 
 def solution(mesh):
@@ -432,29 +453,42 @@
         dma = pltpu.SemaphoreType.DMA
         tile = (8, ey)
         sends = 2 + 8 + 12 + 8
-        return pl.pallas_call(
+        w, cw, hm = pl.pallas_call(
             functools.partial(kernel, sizes),
             out_shape=(
-                jax.ShapeDtypeStruct((NV, ITERS), f32),
-                jax.ShapeDtypeStruct((NV, nodes, ex, ey), f32),
+                pltpu.VMEM((NV, nodes) + tile, f32), pltpu.VMEM((NV,) + tile, f32), pltpu.VMEM(tile, f32),
             ),
-            in_specs=[scalars, scalars] + [hbm] * 5,
-            out_specs=(local, local),
+            in_specs=[hbm] * 7,
+            out_specs=(local, local, local),
             scratch_shapes=[
                 vm((nodes,) + tile, f32), vm((nodes,) + tile, f32), vm((nodes,) + tile, f32), vm(tile, f32),
                 vm((4,) + tile, jnp.int32), vm((4,) + tile, f32),
-                vm((NV + 1, nodes) + tile, f32), vm((nodes,) + tile, f32), vm((nodes,) + tile, f32), vm(tile, f32),
+                vm((nodes,) + tile, f32), vm((nodes,) + tile, f32), vm((nodes,) + tile, f32), vm(tile, f32),
                 vm((4,) + tile, f32), vm((NV, 8) + tile, f32),
                 vm((2, 9) + tile, f32), vm((9,) + tile, f32), vm((9,) + tile, f32),
                 vm((2, 2) + tile, f32), vm((2, 2) + tile, f32), vm((2, 2) + tile, f32), vm((1, 2) + tile, f32),
                 vm((2, 2) + tile, f32), vm((4, 8) + tile, f32),
                 vm((1, 128), f32), vm((n1, 1, 128), f32), vm((2, 128), f32), vm((n2, 2, 128), f32),
-                dma((8,)), dma((sends,)), dma((sends,)), dma((n1,)), dma((n1,)), dma((n2,)), dma((n2,)),
+                pltpu.SMEM((P_SIZE, P_SIZE), f32), pltpu.SMEM((P_SIZE,), f32),
+                dma((10,)), dma((sends,)), dma((sends,)), dma((n1,)), dma((n1,)), dma((n2,)), dma((n2,)),
             ],
             compiler_params=pltpu.CompilerParams(
                 collective_id=0, has_side_effects=True, vmem_limit_bytes=48 * 1024 * 1024),
             name="arnoldi",
-        )(line_op, face_deriv, source, initial, reaction, stiffness, wall_flags)
+        )(*[pltpu.with_memory_space_constraint(t, pltpu.HBM) for t in (
+            line_op, face_deriv, source, initial, reaction, stiffness, wall_flags)])
+        return pl.pallas_call(
+            output_kernel,
+            out_shape=(
+                jax.ShapeDtypeStruct((NV, ITERS), f32),
+                jax.ShapeDtypeStruct((NV, nodes, ex, ey), f32),
+            ),
+            in_specs=[local] * 3,
+            out_specs=(hbm, hbm),
+            scratch_shapes=[vm((NV, ITERS), f32), vm((NV, nodes, ex, ey), f32), dma((NV + 1,))],
+            compiler_params=pltpu.CompilerParams(vmem_limit_bytes=16 * 1024 * 1024),
+            name="combine",
+        )(w, cw, hm)
 
     placed = (P(None, gxs, gys), P(None, gxs, gys), P(None, gxs, gys), P(gxs, gys), P(), P(), P(None, gxs, gys))
     return jax.shard_map(

time: 41.9 us -> 34.6 us (0.83)
  local copies, waits for them, and re-layouts: 6.9 us -> 0 us
    unnamed x16 -> x0, local copies, waits for them, and re-layouts: 6.9 us -> none
    pallas_call x1 -> x2, Pallas kernels: 34.1 us -> 33.9 us  [the longest x1 32.6 us: body(): pl.pallas_call(functools.partial(kernel, sizes), out_shape=(pltpu.VMEM((N...]
where the time goes in v3:
time: 34.6 us; the launch traced here: 34.5 us
  Pallas kernels  33.9 us (98%)
  between operations  0.64 us (2%)
    pallas_call x1, Pallas kernels, body(): pl.pallas_call(functools.partial(kernel, sizes), out_shape=(pltpu.VMEM((N...  32.6 us
    pallas_call x1, Pallas kernels, body(): pl.pallas_call(output_kernel, out_shape=(jax.ShapeDtypeStruct((NV, ITERS)...  1.28 us

profile of v3, /device:TPU:1, one launch (start us, length us, event | category | flops | bytes accessed | tf_op | source)
XLA Modules:
  0.0 34.5 jit_solution(16102106581049752834)
XLA Ops:
  0.6 32.6 %arnoldi.1 = (f32[6,64,8,128]{3,2,1,0:T(8,128)S(1)}, f32[6,8,128]{2,1,0:T(8,128)S(1)}, f32[8,128]{1,0:T(8,128)S(1)}) custom-call(f32[8,8]{1,0:T(8,128)} %line_h.1, f32[8]{0:T(128)} %fd_h.1, f32[64,4,128]{2,1,0:T(4,128)} %src_h.1, f32[64,4,128]{2,1,0:T(4,128)} %x0_h.1, f32[64,4,128]{2,1,0:T(4,128)} %rx_h.1, f32[4,128]{1,0:T(4,128)} %st_h.1, s32[4,4,128]{2,1,0:T(4,128)} %wf_h.1), custom_call_target="tpu_custom_call" | custom-call | tf_op jit(solution)/shard_map/arnoldi/pallas_call | solution.py:456
  33.2 1.3 %combine.1 = (f32[6,5]{1,0:T(8,128)}, f32[6,64,4,128]{3,2,1,0:T(4,128)}) custom-call(f32[6,64,8,128]{3,2,1,0:T(8,128)S(1)} %get-tuple-element.5.w, f32[6,8,128]{2,1,0:T(8,128)S(1)} %get-tuple-element.6.cw, f32[8,128]{1,0:T(8,128)S(1)} %get-tuple-element.7.hm), custom_call_target="tpu_custom_call" | custom-call | tf_op jit(solution)/shard_map/combine/pallas_call | solution.py:480

commit v4 on v3

--- a/solution.py
+++ b/solution.py
@@ -24,11 +24,6 @@
     return s, (a - (s - t)) + (b - t)
 
 
-def quick(a, b):
-    s = a + b
-    return s, b - (s - a)
-
-
 def split(a):
     c = a * 4097.0
     hi = c - (c - a)
@@ -44,17 +39,21 @@
 
 def add2(a, b):
     s, e = two_sum(a[0], b[0])
-    return quick(s, e + (a[1] + b[1]))
+    return s, e + (a[1] + b[1])
 
 
 def mul2(a, b):
     p, e = two_prod(a[0], b[0])
-    return quick(p, e + (a[0] * b[1] + a[1] * b[0]))
+    return p, e + (a[0] * b[1] + a[1] * b[0])
 
 
 def mul1(a, b):
     p, e = two_prod(a[0], b)
-    return quick(p, e + a[1] * b)
+    return p, e + a[1] * b
+
+
+def tidy(a):
+    return two_sum(*a)
 
 
 def tree(items, op):
@@ -70,11 +69,11 @@
 def sublane_total(a):
     for s in (4, 2, 1):
         a = add2(a, tuple(pltpu.roll(v, s, 0) for v in a))
-    return a
-
-
-def kernel(sizes, line_h, fd_h, src_h, x0_h, rx_h, st_h, wf_h, w, cw, hm,
-           xl, sl, rl, stl, wfl, opl, x0, sv, rx, st, op, gw, pk, lb, rb, qs, qr, gqs, gql, gqr, qf,
+    return tidy(a)
+
+
+def kernel(sizes, line_h, fd_h, src_h, x0_h, rx_h, st_h, wf_h, wp, cw, hm,
+           xl, sl, rl, stl, wfl, opl, w, x0, sv, rx, st, op, gw, pk, lb, rb, qs, qr, gqs, gql, gqr, qf,
            row1, buf1, row2, buf2, line, fd,
            lsem, hs, hr, s1, r1, s2, r2):
     ny, nc, nx, nz = sizes
@@ -85,11 +84,10 @@
         j = lax.rem(x * nz + z + nx * nz + dy, nx * nz)
         return (i // nc, lax.rem(i, nc), j // nz, lax.rem(j, nz))
 
-    group1 = [
-        (lax.rem(y + i, ny), lax.rem(c + j, nc), lax.rem(x + k, nx), z)
-        for i in range(ny) for j in range(nc) for k in range(nx) if i + j + k > 0
-    ]
-    group2 = [(y, c, x, lax.rem(z + k, nz)) for k in range(1, nz)]
+    hub = c == nc - 1
+    plane = [(lax.rem(y + i, ny), lax.rem(x + k, nx)) for i in range(ny) for k in range(nx)]
+    planes = [lax.rem(z + k, nz) for k in range(1, nz)]
+    me = (c * ny + y) * nx + x
     around = {(i, j): at(i, j) for i in (-1, 0, 1) for j in (-1, 0, 1) if (i, j) != (0, 0)}
     own = pl.ds(0, 4)
     pairs = [(line_h, line), (fd_h, fd), (x0_h, xl.at[:, own, :]), (rx_h, rl.at[:, own, :]), (src_h, sl.at[:, own, :]), (st_h, stl.at[own, :]),
@@ -99,9 +97,23 @@
         cp.start()
 
     barrier = pltpu.get_barrier_semaphore()
-    greeted = list(around.values()) + group1 + group2
-    for peer in greeted:
+    def greet(peer):
         pl.semaphore_signal(barrier, inc=1, device_id=peer, device_id_type=MESH)
+
+    for peer in around.values():
+        greet(peer)
+    for i, (yy, xx) in enumerate(plane):
+        greet((yy, nc - 1, xx, z) if i else (y, nc - 1 - c, x, z))
+    for zz in planes:
+        greet((y, nc - 1, x, zz))
+
+    @pl.when(hub)
+    def _():
+        for yy, xx in plane[1:]:
+            greet((yy, 0, xx, z))
+        for zz in planes:
+            greet((y, 0, x, zz))
+
     for cp in loads[:2]:
         cp.wait()
     n = P_SIZE
@@ -163,7 +175,14 @@
     pst = gather_groups([stl[...]] + [opl[f] for f in range(4)], 6)
     pk[0, n] = pst
     pk[1, n] = pst
-    pl.semaphore_wait(barrier, len(greeted))
+    @pl.when(hub)
+    def _():
+        pl.semaphore_wait(barrier, 8 + 31 + 14)
+
+    @pl.when(jnp.logical_not(hub))
+    def _():
+        pl.semaphore_wait(barrier, 8 + 16 + 7)
+
 
     def send(copies, peer, pieces, first):
         for i, (a, b) in enumerate(pieces):
@@ -222,17 +241,11 @@
     for side in (0, 1):
         gqr[0, side] = jnp.where(before_half, gql[0, side], gqr[0, side])
 
-    def apply(k, last=False, fresh=None):
+    def apply(k, last=False, fresh=None, after_strip=None, after_half=None):
         wide = k != 2
 
         def v(a, b):
             return w[k - 1, a * n + b] if k else x0[a * n + b]
-
-        def keep(a, b, t):
-            if wide:
-                w[k, a * n + b] = t
-            else:
-                w[k, a * n + b, 0:4, :] = t[0:4, :]
 
         gv = [gw[k, b] for b in range(n)]
         gqsouth = tree([g[i] * gv[i] for i in range(n)], jnp.add)
@@ -267,61 +280,89 @@
                     gw[k + 1, b] = t
                 else:
                     gw[k + 1, b, 0:4, :] = t[0:4, :]
-        stiff = st[...]
+            if after_strip is not None:
+                after_strip()
         for b in range(n):
-            col = [v(i, b) for i in range(n)]
-            qwest = tree([g[i] * col[i] for i in range(n)], jnp.add)
-            qeast = tree([g[i] * col[n - 1 - i] for i in range(n)], jnp.add)
+            qwest = tree([g[i] * v(i, b) for i in range(n)], jnp.add)
+            qeast = tree([g[i] * v(n - 1 - i, b) for i in range(n)], jnp.add)
             prev = pltpu.roll(qeast, 1, 0)
             nxt = pltpu.roll(qwest, 7, 0)
             if fresh is not None:
                 prev = jnp.where(sub == 6, jnp.broadcast_to(qr[fresh, 1, pl.ds(b, 1), :], (8, 128)), prev)
                 nxt = jnp.where(sub == 5, jnp.broadcast_to(qr[fresh, 0, pl.ds(b, 1), :], (8, 128)), nxt)
-            for a in range(n):
-                acc = tree([lop[a][i] * col[i] for i in range(n)] + [lop[b][i] * v(a, i) for i in range(n)], jnp.add)
+            qf[0, b] = qwest - op[0] * prev
+            qf[1, b] = qeast - op[1] * nxt
+        stiff = st[...]
+        for a in range(n):
+            row = [v(a, i) for i in range(n)]
+            even = None
+            for b in range(n):
+                acc = tree([lop[b][i] * row[i] for i in range(n)] + [lop[a][i] * v(i, b) for i in range(n)], jnp.add)
                 if k == 0:
-                    t = rx[a * n + b] * col[a] - sv[a * n + b] + stiff * acc
+                    t = rx[a * n + b] * row[b] - sv[a * n + b] + stiff * acc
                 else:
-                    t = (rx[a * n + b] - shift) * col[a] + stiff * acc
+                    t = (rx[a * n + b] - shift) * row[b] + stiff * acc
                 if a == 0:
-                    t = t + (qwest - op[0] * prev)
+                    t = t + qf[0, b]
                 if a == n - 1:
-                    t = t + (qeast - op[1] * nxt)
+                    t = t + qf[1, b]
                 if b == 0:
                     t = t + qf[2, a]
                 if b == n - 1:
                     t = t + qf[3, a]
-                keep(a, b, t)
+                if k == 2:
+                    w[k, a * n + b, 0:4, :] = t[0:4, :]
+                elif not last:
+                    w[k, a * n + b] = t
+                if b % 2 == 0:
+                    even = t
+                else:
+                    wp[k, (a * n + b) // 2] = jnp.where(sub < 4, even, pltpu.roll(t, 4, 0))
+            if a == 3 and after_half is not None:
+                after_half()
 
     apply(0, fresh=0)
     apply(1)
-    apply(2)
+    copies = []
+    sides = ((1, 2, 6), (-1, 0, 4))
+
+    def send_strip():
+        nonlocal used
+        for b in range(n):
+            t = jnp.concatenate([gw[3, b, 0:4, :]] * 2, axis=0)
+            face = strip_faces(t)[1]
+            gqs[1, 0, pl.ds(b, 1), :] = face[2:3, :]
+            gqs[1, 1, pl.ds(b, 1), :] = face[1:2, :]
+        for dx, lo, to in sides:
+            side = 1 if dx > 0 else 0
+            used = send(copies, around[dx, 0], [
+                (gw.at[3, :, rows(lo), :], gw.at[3, :, rows(to), :]), (gqs.at[1, side], gqr.at[1, side])], used)
+
+    def send_block(first):
+        nonlocal used
+        part = pl.ds(first, n * n // 2)
+        for dx, lo, to in sides:
+            used = send(copies, around[dx, 0], [(w.at[2, part, rows(lo), :], w.at[2, part, rows(to), :])], used)
+
+    apply(2, after_strip=send_strip, after_half=lambda: send_block(0))
+    send_block(n * n // 2)
     qw, qe = x_faces(lambda a, b: w[2, a * n + b, 0:4, :])
     for b in range(n):
         qs[1, 0, pl.ds(b, 1), :] = qw[b][2:3, :]
         qs[1, 1, pl.ds(b, 1), :] = qe[b][1:2, :]
-        t = jnp.concatenate([gw[3, b, 0:4, :]] * 2, axis=0)
-        face = strip_faces(t)[1]
-        gqs[1, 0, pl.ds(b, 1), :] = face[2:3, :]
-        gqs[1, 1, pl.ds(b, 1), :] = face[1:2, :]
-    copies = []
-    for dx, lo, to in ((1, 2, 6), (-1, 0, 4)):
+    for dx, lo, to in sides:
         side = 1 if dx > 0 else 0
-        used = send(copies, around[dx, 0], [
-            (w.at[2, :, rows(lo), :], w.at[2, :, rows(to), :]),
-            (gw.at[3, :, rows(lo), :], gw.at[3, :, rows(to), :]),
-            (qs.at[1, side], qr.at[1, side]),
-            (gqs.at[1, side], gqr.at[1, side])], used)
+        used = send(copies, around[dx, 0], [(qs.at[1, side], qr.at[1, side])], used)
     def gram(pairs):
         top = max(j for i, j in pairs) + 1
 
         def body(q, acc):
-            vals = [w[i, q] for i in range(top)]
+            vals = [wp[i, q] for i in range(top)]
             return tuple(t + vals[i] * vals[j] for t, (i, j) in zip(acc, pairs))
 
-        return lax.fori_loop(0, n * n, body, tuple(jnp.zeros((8, 128), jnp.float32) for _ in pairs), unroll=2)
-
-    early = [p for p in PAIRS if p[1] < 2]
+        return lax.fori_loop(0, n * n // 2, body, tuple(jnp.zeros((8, 128), jnp.float32) for _ in pairs), unroll=8)
+
+    early = [p for p in PAIRS if p[1] < 3]
     first = gram(early)
     for cp in copies:
         cp.wait()
@@ -334,7 +375,6 @@
     for base in range(0, len(PAIRS), 8):
         packed = jnp.zeros((8, 128), jnp.float32)
         for i, t in enumerate(acc[base:base + 8]):
-            t = jnp.where(sub < 4, t, 0.0)
             t = t + pltpu.roll(t, 4, 0)
             t = t + pltpu.roll(t, 2, 0)
             t = t + pltpu.roll(t, 1, 0)
@@ -343,28 +383,60 @@
         line_row = line_row + jnp.where(lane == sub + base, packed, 0.0)
     for s in (4, 2, 1):
         line_row = line_row + pltpu.roll(line_row, s, 0)
+    zero1 = jnp.zeros((1, 128), jnp.float32)
     row1[...] = line_row[0:1, :]
-    copies = []
-    for j, peer in enumerate(group1):
-        cp = pltpu.make_async_remote_copy(
-            src_ref=row1, dst_ref=buf1.at[j], send_sem=s1.at[j], recv_sem=r1.at[j], device_id=peer, device_id_type=MESH)
-        cp.start()
-        copies.append(cp)
-    for cp in copies:
-        cp.wait()
-    zero1 = jnp.zeros((1, 128), jnp.float32)
-    part = tree([(row1[...], zero1)] + [(buf1[j], zero1) for j in range(len(group1))], add2)
-    row2[0:1, :] = part[0]
-    row2[1:2, :] = part[1]
-    copies = []
-    for j, peer in enumerate(group2):
-        cp = pltpu.make_async_remote_copy(
-            src_ref=row2, dst_ref=buf2.at[j], send_sem=s2.at[j], recv_sem=r2.at[j], device_id=peer, device_id_type=MESH)
-        cp.start()
-        copies.append(cp)
-    for cp in copies:
-        cp.wait()
-    part = tree([part] + [(buf2[j, 0:1, :], buf2[j, 1:2, :]) for j in range(len(group2))], add2)
+
+    def to_hub(j, index, peer):
+        return pltpu.make_async_remote_copy(
+            src_ref=row1, dst_ref=buf1.at[index], send_sem=s1.at[j], recv_sem=r1.at[index],
+            device_id=peer, device_id_type=MESH)
+
+    def across(j, index, peer):
+        return pltpu.make_async_remote_copy(
+            src_ref=row2, dst_ref=buf2.at[index], send_sem=s2.at[j], recv_sem=r2.at[index],
+            device_id=peer, device_id_type=MESH)
+
+    partner = (y, nc - 1 - c, x, z)
+    for j, (yy, xx) in enumerate(plane):
+        if j:
+            to_hub(j, me, (yy, nc - 1, xx, z)).start()
+
+    @pl.when(hub)
+    def _():
+        buf1[me] = row1[...]
+        for j, (yy, xx) in enumerate(plane):
+            for cc in range(nc):
+                if j or cc != nc - 1:
+                    to_hub(j, (cc * ny + yy) * nx + xx, partner).wait_recv()
+        total1 = tree([(buf1[j], zero1) for j in range(nc * ny * nx)], add2)
+        total1 = tidy(total1)
+        row2[0:1, :] = total1[0]
+        row2[1:2, :] = total1[1]
+        k = 0
+        for zz in planes:
+            for cc in (nc - 1, 0):
+                across(k, z, (y, cc, x, zz)).start()
+                k += 1
+        across(k, z, partner).start()
+        buf2[z] = row2[...]
+
+    @pl.when(jnp.logical_not(hub))
+    def _():
+        to_hub(0, me, partner).start()
+        across(0, z, partner).wait_recv()
+        to_hub(0, me, partner).wait_send()
+
+    for zz in planes:
+        across(0, zz, partner).wait_recv()
+    for j in range(1, len(plane)):
+        to_hub(j, me, partner).wait_send()
+
+    @pl.when(hub)
+    def _():
+        for k in range(2 * len(planes) + 1):
+            across(k, z, partner).wait_send()
+
+    part = tidy(tree([(buf2[j, 0:1, :], buf2[j, 1:2, :]) for j in range(nz)], add2))
 
     slot = {}
     for p, (i, j) in enumerate(PAIRS):
@@ -382,41 +454,47 @@
     def spread(t, k):
         return jnp.broadcast_to(t[k:k + 1, :], (8, 128))
 
-    def times_gram(u):
-        return tree([mul2(columns[k], tuple(spread(t, k) for t in u)) for k in range(NV)], add2)
-
     def dot(a, b):
         return sublane_total(mul2(a, b))
 
+    wide_shift = jnp.broadcast_to(shift, (8, 128))
+    moved = [add2(columns[k + 1], mul1(columns[k], wide_shift)) for k in range(ITERS)]
+    moved = [tidy(t) for t in moved]
     hmat = jnp.zeros((8, 128), jnp.float32)
     zeros = jnp.zeros((8, 128), jnp.float32)
     u = (jnp.where(sub == 0, -1.0, 0.0), zeros)
-    e = times_gram(u)
+    e = tuple(-t for t in columns[0])
+    ratio = None
     coefs, images = [], []
     for j in range(NV):
-        square = dot(u, e)[0] + FLOOR
+        square = dot(u, e)[0]
+        square = (square if ratio is None else square * (ratio * ratio)) + FLOOR
         inv = lax.rsqrt(square)
         if j > 0:
             hmat = jnp.where((sub == j) & (lane == j - 1), square * inv, hmat)
-        coefs.append(mul1(u, inv))
-        images.append(mul1(e, inv))
+        unit = inv if ratio is None else inv * ratio
+        coefs.append(tidy(mul1(u, unit)))
         if j == ITERS:
             break
-        moved = tuple(pltpu.roll(t, 1, 0) for t in coefs[j])
-        u = add2(moved, mul1(coefs[j], jnp.broadcast_to(shift, (8, 128))))
-        e = times_gram(u)
-        hs_j = [dot(images[i], u)[0] for i in range(j + 1)]
-        for i in range(j + 1):
-            hmat = jnp.where((sub == i) & (lane == j), hs_j[i], hmat)
-        u = tree([u] + [mul1(coefs[i], -hs_j[i]) for i in range(j + 1)], add2)
-        e = tree([e] + [mul1(images[i], -hs_j[i]) for i in range(j + 1)], add2)
+        images.append(tidy(mul1(e, unit)))
+        m = tidy(add2(tuple(pltpu.roll(t, 1, 0) for t in u), mul1(u, wide_shift)))
+        f = tree([mul2(moved[k], tuple(spread(t, k) for t in u)) for k in range(j + 1)], add2)
+        parts = [dot(images[i], m)[0] for i in range(j)]
+        own = dot(e, m)[0] * (unit * unit)
+        for i in range(j):
+            hmat = jnp.where((sub == i) & (lane == j), parts[i] * unit, hmat)
+        hmat = jnp.where((sub == j) & (lane == j), own, hmat)
+        u, e = (
+            tidy(tree([x] + [mul1(basis[i], -parts[i]) for i in range(j)] + [mul1(latest, -own)], add2))
+            for x, basis, latest in ((m, coefs, u), (f, images, e)))
+        ratio = unit
     hm[...] = hmat
     for j in range(NV):
         cw[j] = coefs[j][0]
 
 
 def output_kernel(w, cw, hm, hess_h, out_h, hess, vout, sem):
-    nodes = w.shape[1]
+    half = w.shape[1]
     hess[...] = hm[0:NV, 0:ITERS]
     outs = [pltpu.make_async_copy(hess, hess_h, sem.at[0])]
     outs[0].start()
@@ -425,10 +503,11 @@
 
         def combine(q, carry):
             t = tree([weights[i] * w[i, q] for i in range(j + 1)], jnp.add)
-            vout[j, q] = t[0:4, :]
+            vout[j, 2 * q] = t[0:4, :]
+            vout[j, 2 * q + 1] = t[4:8, :]
             return carry
 
-        lax.fori_loop(0, nodes, combine, 0, unroll=8)
+        lax.fori_loop(0, half, combine, 0, unroll=8)
         cp = pltpu.make_async_copy(vout.at[j], out_h.at[j], sem.at[j + 1])
         cp.start()
         outs.append(cp)
@@ -445,32 +524,31 @@
 
     def body(source, initial, reaction, stiffness, line_op, face_deriv, wall_flags):
         nodes, ex, ey = source.shape
-        n1, n2 = ny * nc * nx - 1, nz - 1
         hbm = pl.BlockSpec(memory_space=pltpu.HBM)
         scalars = pl.BlockSpec(memory_space=pltpu.SMEM)
         local = pl.BlockSpec(memory_space=pltpu.VMEM)
         vm = pltpu.VMEM
         dma = pltpu.SemaphoreType.DMA
         tile = (8, ey)
-        sends = 2 + 8 + 12 + 8
+        sends = 2 + 8 + 12 + 10
         w, cw, hm = pl.pallas_call(
             functools.partial(kernel, sizes),
             out_shape=(
-                pltpu.VMEM((NV, nodes) + tile, f32), pltpu.VMEM((NV,) + tile, f32), pltpu.VMEM(tile, f32),
+                pltpu.VMEM((NV, nodes // 2) + tile, f32), pltpu.VMEM((NV,) + tile, f32), pltpu.VMEM(tile, f32),
             ),
             in_specs=[hbm] * 7,
             out_specs=(local, local, local),
             scratch_shapes=[
                 vm((nodes,) + tile, f32), vm((nodes,) + tile, f32), vm((nodes,) + tile, f32), vm(tile, f32),
                 vm((4,) + tile, jnp.int32), vm((4,) + tile, f32),
-                vm((nodes,) + tile, f32), vm((nodes,) + tile, f32), vm((nodes,) + tile, f32), vm(tile, f32),
-                vm((4,) + tile, f32), vm((NV, 8) + tile, f32),
+                vm((NV - 1, nodes) + tile, f32), vm((nodes,) + tile, f32), vm((nodes,) + tile, f32), vm((nodes,) + tile, f32),
+                vm(tile, f32), vm((4,) + tile, f32), vm((NV, 8) + tile, f32),
                 vm((2, 9) + tile, f32), vm((9,) + tile, f32), vm((9,) + tile, f32),
                 vm((2, 2) + tile, f32), vm((2, 2) + tile, f32), vm((2, 2) + tile, f32), vm((1, 2) + tile, f32),
                 vm((2, 2) + tile, f32), vm((4, 8) + tile, f32),
-                vm((1, 128), f32), vm((n1, 1, 128), f32), vm((2, 128), f32), vm((n2, 2, 128), f32),
+                vm((1, 128), f32), vm((nc * ny * nx, 1, 128), f32), vm((2, 128), f32), vm((nz, 2, 128), f32),
                 pltpu.SMEM((P_SIZE, P_SIZE), f32), pltpu.SMEM((P_SIZE,), f32),
-                dma((10,)), dma((sends,)), dma((sends,)), dma((n1,)), dma((n1,)), dma((n2,)), dma((n2,)),
+                dma((10,)), dma((sends,)), dma((sends,)), dma((ny * nx,)), dma((nc * ny * nx,)), dma((2 * nz - 1,)), dma((nz,)),
             ],
             compiler_params=pltpu.CompilerParams(
                 collective_id=0, has_side_effects=True, vmem_limit_bytes=48 * 1024 * 1024),

time: 34.6 us -> 33.5 us (0.968)
  Pallas kernels: 33.9 us -> 32.7 us
    pallas_call x1, Pallas kernels: 32.6 us -> 31.7 us  [body(): pl.pallas_call(functools.partial(kernel, sizes), out_shape=(pltpu.VMEM((N...]
where the time goes in v4:
time: 33.5 us; the launch traced here: 33.4 us
  Pallas kernels  32.7 us (98%)
  between operations  0.64 us (2%)
    pallas_call x1, Pallas kernels, body(): pl.pallas_call(functools.partial(kernel, sizes), out_shape=(pltpu.VMEM((N...  31.7 us
    pallas_call x1, Pallas kernels, body(): pl.pallas_call(output_kernel, out_shape=(jax.ShapeDtypeStruct((NV, ITERS)...  1 us

profile of v4, /device:TPU:1, one launch (start us, length us, event | category | flops | bytes accessed | tf_op | source)
XLA Modules:
  0.0 33.4 jit_solution(12819610693571819450)
XLA Ops:
  0.6 31.7 %arnoldi.1 = (f32[6,32,8,128]{3,2,1,0:T(8,128)S(1)}, f32[6,8,128]{2,1,0:T(8,128)S(1)}, f32[8,128]{1,0:T(8,128)S(1)}) custom-call(f32[8,8]{1,0:T(8,128)} %line_h.1, f32[8]{0:T(128)} %fd_h.1, f32[64,4,128]{2,1,0:T(4,128)} %src_h.1, f32[64,4,128]{2,1,0:T(4,128)} %x0_h.1, f32[64,4,128]{2,1,0:T(4,128)} %rx_h.1, f32[4,128]{1,0:T(4,128)} %st_h.1, s32[4,4,128]{2,1,0:T(4,128)} %wf_h.1), custom_call_target="tpu_custom_call" | custom-call | tf_op jit(solution)/shard_map/arnoldi/pallas_call | solution.py:534
  32.4 1.0 %combine.1 = (f32[6,5]{1,0:T(8,128)}, f32[6,64,4,128]{3,2,1,0:T(4,128)}) custom-call(f32[6,32,8,128]{3,2,1,0:T(8,128)S(1)} %get-tuple-element.5.w, f32[6,8,128]{2,1,0:T(8,128)S(1)} %get-tuple-element.6.cw, f32[8,128]{1,0:T(8,128)S(1)} %get-tuple-element.7.hm), custom_call_target="tpu_custom_call" | custom-call | tf_op jit(solution)/shard_map/combine/pallas_call | solution.py:558

commit v5 on v4

--- a/solution.py
+++ b/solution.py
@@ -74,7 +74,7 @@
 
 def kernel(sizes, line_h, fd_h, src_h, x0_h, rx_h, st_h, wf_h, wp, cw, hm,
            xl, sl, rl, stl, wfl, opl, w, x0, sv, rx, st, op, gw, pk, lb, rb, qs, qr, gqs, gql, gqr, qf,
-           row1, buf1, row2, buf2, line, fd,
+           row1, buf1, row2, buf2, line, fd, rxp, cpair,
            lsem, hs, hr, s1, r1, s2, r2):
     ny, nc, nx, nz = sizes
     y, c, x, z = (lax.axis_index(a) for a in AXES)
@@ -97,22 +97,27 @@
         cp.start()
 
     barrier = pltpu.get_barrier_semaphore()
+
     def greet(peer):
         pl.semaphore_signal(barrier, inc=1, device_id=peer, device_id_type=MESH)
 
+    far = sorted(range(1, nz), key=lambda k: -min(k, nz - k))
+    flat = sorted(range(1, ny * nx), key=lambda i: -min(i // nx, ny - i // nx) - min(i % nx, nx - i % nx))
+    for k in far:
+        greet((y, nc - 1, x, planes[k - 1]))
+    for i in flat:
+        greet((plane[i][0], nc - 1, plane[i][1], z))
+
+    @pl.when(hub)
+    def _():
+        for k in far:
+            greet((y, 0, x, planes[k - 1]))
+        for i in flat:
+            greet((plane[i][0], 0, plane[i][1], z))
+
     for peer in around.values():
         greet(peer)
-    for i, (yy, xx) in enumerate(plane):
-        greet((yy, nc - 1, xx, z) if i else (y, nc - 1 - c, x, z))
-    for zz in planes:
-        greet((y, nc - 1, x, zz))
-
-    @pl.when(hub)
-    def _():
-        for yy, xx in plane[1:]:
-            greet((yy, 0, xx, z))
-        for zz in planes:
-            greet((y, 0, x, zz))
+    greet((y, nc - 1 - c, x, z))
 
     for cp in loads[:2]:
         cp.wait()
@@ -215,6 +220,8 @@
             (qs.at[0, side], qr.at[0, side])], used)
     st[0:4, :] = stl[0:4, :]
     op[:, 0:4, :] = opl[:, 0:4, :]
+    for q in range(0, n * n, 2):
+        rxp[q // 2] = jnp.where(sub < 4, rl[q], pltpu.roll(rl[q + 1], 4, 0)) - shift
     for cp in loads[7:]:
         cp.wait()
     for cp in copies:
@@ -240,6 +247,15 @@
     gops, gopn = spreads[3], spreads[4]
     for side in (0, 1):
         gqr[0, side] = jnp.where(before_half, gql[0, side], gqr[0, side])
+
+    low = sub < 4
+    for j in range(n // 2):
+        for i in range(n // 2):
+            cpair[0, j * 4 + i] = jnp.where(low, lop[2 * j][2 * i], lop[2 * j + 1][2 * i + 1])
+            cpair[1, j * 4 + i] = jnp.where(low, lop[2 * j][2 * i + 1], lop[2 * j + 1][2 * i])
+
+    def pair_up(even, odd):
+        return jnp.where(low, even, pltpu.roll(odd, 4, 0))
 
     def apply(k, last=False, fresh=None, after_strip=None, after_half=None):
         wide = k != 2
@@ -292,6 +308,32 @@
                 nxt = jnp.where(sub == 5, jnp.broadcast_to(qr[fresh, 0, pl.ds(b, 1), :], (8, 128)), nxt)
             qf[0, b] = qwest - op[0] * prev
             qf[1, b] = qeast - op[1] * nxt
+        if not wide or last:
+            stiff = pair_up(st[...], st[...])
+            for a in range(n):
+                tiles = [wp[k - 1, a * 4 + j] for j in range(4)]
+                swapped = [pltpu.roll(t, 4, 0) for t in tiles]
+                for j in range(4):
+                    q = a * n + 2 * j
+                    acc = tree([lop[a][i] * wp[k - 1, i * 4 + j] for i in range(n)]
+                               + [cpair[0, j * 4 + i] * tiles[i] for i in range(4)]
+                               + [cpair[1, j * 4 + i] * swapped[i] for i in range(4)], jnp.add)
+                    t = rxp[q // 2] * tiles[j] + stiff * acc
+                    if a == 0:
+                        t = t + pair_up(qf[0, 2 * j], qf[0, 2 * j + 1])
+                    if a == n - 1:
+                        t = t + pair_up(qf[1, 2 * j], qf[1, 2 * j + 1])
+                    if j == 0:
+                        t = t + jnp.where(low, qf[2, a], 0.0)
+                    if j == 3:
+                        t = t + jnp.where(low, 0.0, pltpu.roll(qf[3, a], 4, 0))
+                    wp[k, q // 2] = t
+                    if not last:
+                        w[k, q, 0:4, :] = t[0:4, :]
+                        w[k, q + 1, 0:4, :] = pltpu.roll(t, 4, 0)[0:4, :]
+                if a == 3 and after_half is not None:
+                    after_half()
+            return
         stiff = st[...]
         for a in range(n):
             row = [v(a, i) for i in range(n)]
@@ -310,16 +352,11 @@
                     t = t + qf[2, a]
                 if b == n - 1:
                     t = t + qf[3, a]
-                if k == 2:
-                    w[k, a * n + b, 0:4, :] = t[0:4, :]
-                elif not last:
-                    w[k, a * n + b] = t
+                w[k, a * n + b] = t
                 if b % 2 == 0:
                     even = t
                 else:
-                    wp[k, (a * n + b) // 2] = jnp.where(sub < 4, even, pltpu.roll(t, 4, 0))
-            if a == 3 and after_half is not None:
-                after_half()
+                    wp[k, (a * n + b) // 2] = pair_up(even, t)
 
     apply(0, fresh=0)
     apply(1)
@@ -548,6 +585,7 @@
                 vm((2, 2) + tile, f32), vm((4, 8) + tile, f32),
                 vm((1, 128), f32), vm((nc * ny * nx, 1, 128), f32), vm((2, 128), f32), vm((nz, 2, 128), f32),
                 pltpu.SMEM((P_SIZE, P_SIZE), f32), pltpu.SMEM((P_SIZE,), f32),
+                vm((nodes // 2,) + tile, f32), vm((2, 16) + tile, f32),
                 dma((10,)), dma((sends,)), dma((sends,)), dma((ny * nx,)), dma((nc * ny * nx,)), dma((2 * nz - 1,)), dma((nz,)),
             ],
             compiler_params=pltpu.CompilerParams(

time: 33.5 us -> 32.9 us (0.982)
  Pallas kernels: 32.7 us -> 32.2 us
    pallas_call x1, Pallas kernels: 31.7 us -> 31.2 us  [body(): pl.pallas_call(functools.partial(kernel, sizes), out_shape=(pltpu.VMEM((N...]
where the time goes in v5:
time: 32.9 us; the launch traced here: 32.8 us
  Pallas kernels  32.2 us (98%)
  between operations  0.64 us (2%)
    pallas_call x1, Pallas kernels, body(): pl.pallas_call(functools.partial(kernel, sizes), out_shape=(pltpu.VMEM((N...  31.2 us
    pallas_call x1, Pallas kernels, body(): pl.pallas_call(output_kernel, out_shape=(jax.ShapeDtypeStruct((NV, ITERS)...  1 us

profile of v5, /device:TPU:1, one launch (start us, length us, event | category | flops | bytes accessed | tf_op | source)
XLA Modules:
  0.0 32.8 jit_solution(14552278019760032331)
XLA Ops:
  0.6 31.2 %arnoldi.1 = (f32[6,32,8,128]{3,2,1,0:T(8,128)S(1)}, f32[6,8,128]{2,1,0:T(8,128)S(1)}, f32[8,128]{1,0:T(8,128)S(1)}) custom-call(f32[8,8]{1,0:T(8,128)} %line_h.1, f32[8]{0:T(128)} %fd_h.1, f32[64,4,128]{2,1,0:T(4,128)} %src_h.1, f32[64,4,128]{2,1,0:T(4,128)} %x0_h.1, f32[64,4,128]{2,1,0:T(4,128)} %rx_h.1, f32[4,128]{1,0:T(4,128)} %st_h.1, s32[4,4,128]{2,1,0:T(4,128)} %wf_h.1), custom_call_target="tpu_custom_call" | custom-call | tf_op jit(solution)/shard_map/arnoldi/pallas_call | solution.py:571
  31.8 1.0 %combine.1 = (f32[6,5]{1,0:T(8,128)}, f32[6,64,4,128]{3,2,1,0:T(4,128)}) custom-call(f32[6,32,8,128]{3,2,1,0:T(8,128)S(1)} %get-tuple-element.5.w, f32[6,8,128]{2,1,0:T(8,128)S(1)} %get-tuple-element.6.cw, f32[8,128]{1,0:T(8,128)S(1)} %get-tuple-element.7.hm), custom_call_target="tpu_custom_call" | custom-call | tf_op jit(solution)/shard_map/combine/pallas_call | solution.py:596

commit v6 on v5

--- a/solution.py
+++ b/solution.py
@@ -73,8 +73,8 @@
 
 
 def kernel(sizes, line_h, fd_h, src_h, x0_h, rx_h, st_h, wf_h, wp, cw, hm,
-           xl, sl, rl, stl, wfl, opl, w, x0, sv, rx, st, op, gw, pk, lb, rb, qs, qr, gqs, gql, gqr, qf,
-           row1, buf1, row2, buf2, line, fd, rxp, cpair,
+           xl, sl, rl, stl, wfl, opl, w, rx, st, op, gw, pk, lb, rb, qs, qr, gqs, gql, gqr, qf,
+           row1, buf1, row2, buf2, line, fd, rxp, cpair, xc, mm,
            lsem, hs, hr, s1, r1, s2, r2):
     ny, nc, nx, nz = sizes
     y, c, x, z = (lax.axis_index(a) for a in AXES)
@@ -91,7 +91,7 @@
     around = {(i, j): at(i, j) for i in (-1, 0, 1) for j in (-1, 0, 1) if (i, j) != (0, 0)}
     own = pl.ds(0, 4)
     pairs = [(line_h, line), (fd_h, fd), (x0_h, xl.at[:, own, :]), (rx_h, rl.at[:, own, :]), (src_h, sl.at[:, own, :]), (st_h, stl.at[own, :]),
-             (wf_h, wfl.at[:, own, :]), (x0_h, x0.at[:, own, :]), (rx_h, rx.at[:, own, :]), (src_h, sv.at[:, own, :])]
+             (wf_h, wfl.at[:, own, :]), (rx_h, rx.at[:, own, :])]
     loads = [pltpu.make_async_copy(a, b, lsem.at[i]) for i, (a, b) in enumerate(pairs)]
     for cp in loads:
         cp.start()
@@ -166,20 +166,43 @@
         cp.wait()
     opl[...] = 1.0 - wfl[...].astype(jnp.float32)
     qw, qe = x_faces(lambda a, b: xl[a * n + b])
+    qsouth = [tree([g[i] * xl[a * n + i] for i in range(n)], jnp.add) for a in range(n)]
+    qnorth = [tree([g[i] * xl[a * n + n - 1 - i] for i in range(n)], jnp.add) for a in range(n)]
     for b in range(n):
-        qs[0, 0, pl.ds(b, 1), :] = qw[b][2:3, :]
-        qs[0, 1, pl.ds(b, 1), :] = qe[b][1:2, :]
+        qs[0, 0, pl.ds(b, 1), :] = qw[b][0:1, :]
+        qs[0, 1, pl.ds(b, 1), :] = qe[b][3:4, :]
+        gqs[0, 0, pl.ds(b, 1), :] = qw[b][2:3, :]
+        gqs[0, 1, pl.ds(b, 1), :] = qe[b][1:2, :]
+        xc[0, b] = pltpu.roll(qe[b], 1, 0)
+        xc[1, b] = pltpu.roll(qw[b], 7, 0)
+        qf[0, b] = qw[b] - opl[0] * jnp.where(sub == 0, 0.0, xc[0, b])
+        qf[1, b] = qe[b] - opl[1] * jnp.where(sub == 3, 0.0, xc[1, b])
+    for a in range(n):
+        qf[2, a] = qsouth[a] - opl[2] * jnp.where(lane == 0, 0.0, lroll(qnorth[a], 1))
+        qf[3, a] = qnorth[a] - opl[3] * jnp.where(lane == 127, 0.0, lroll(qsouth[a], -1))
+    mm[0, 0:4, :] = gather_groups(qnorth, 7)[0:4, :]
+    mm[1, 0:4, :] = gather_groups(qsouth, 5)[0:4, :]
+    for a in range(n):
+        row = [xl[a * n + i] for i in range(n)]
+        for b in range(n):
+            acc = tree([lop[b][i] * row[i] for i in range(n)] + [lop[a][i] * xl[i * n + b] for i in range(n)], jnp.add)
+            t = rl[a * n + b] * row[b] - sl[a * n + b] + stl[...] * acc
+            for edge, f, i in ((a == 0, 0, b), (a == n - 1, 1, b), (b == 0, 2, a), (b == n - 1, 3, a)):
+                if edge:
+                    t = t + qf[f, i]
+            w[0, a * n + b, 0:4, :] = t[0:4, :]
     for b in range(n):
         px = gather_groups([xl[a * n + b] for a in range(n)], 6)
         ps = gather_groups([sl[a * n + b] for a in range(n)], 6)
         pr = gather_groups([rl[a * n + b] for a in range(n)], 6)
         pk[0, b] = jnp.where(slot16 < 6, px, jnp.where(slot16 < 11, lroll(ps, 5), lroll(pr, 10)))
         pk[1, b] = jnp.where(slot16 < 6, lroll(px, -6), jnp.where(slot16 < 11, ps, lroll(pr, 5)))
-    gqs[0, 0] = lroll(qs[0, 0], 6)
-    gqs[0, 1] = lroll(qs[0, 1], 118)
-    pst = gather_groups([stl[...]] + [opl[f] for f in range(4)], 6)
-    pk[0, n] = pst
-    pk[1, n] = pst
+    gqs[0, 0] = lroll(gqs[0, 0], 6)
+    gqs[0, 1] = lroll(gqs[0, 1], 118)
+    for f, t in enumerate([stl[...]] + [opl[i] for i in range(4)]):
+        spread_out = gather_groups([t] * n, 6)
+        pk[0, n + f] = spread_out
+        pk[1, n + f] = spread_out
     @pl.when(hub)
     def _():
         pl.semaphore_wait(barrier, 8 + 31 + 14)
@@ -212,9 +235,9 @@
     for dx, lo, to in ((1, 2, 6), (-1, 0, 4)):
         side = 1 if dx > 0 else 0
         used = send(copies, around[dx, 0], [
-            (xl.at[:, rows(lo), :], x0.at[:, rows(to), :]),
+            (w.at[0, :, rows(lo), :], w.at[0, :, rows(to), :]),
             (rl.at[:, rows(lo), :], rx.at[:, rows(to), :]),
-            (sl.at[:, rows(lo), :], sv.at[:, rows(to), :]),
+            (mm.at[:, rows(lo), :], mm.at[:, rows(to), :]),
             (stl.at[rows(lo), :], st.at[rows(to), :]),
             (opl.at[:, rows(lo), :], op.at[:, rows(to), :]),
             (qs.at[0, side], qr.at[0, side])], used)
@@ -234,13 +257,7 @@
         gw[0, b] = jnp.where(before_half, lo, lroll(hi, 6))
         gsv.append(jnp.where(before_half, lroll(lo, -5), hi))
         grx.append(jnp.where(before_half, lroll(lo, -10), lroll(hi, -5)))
-    both = jnp.where(before_half, lb[n], rb[n])
-    spreads = []
-    for f in range(5):
-        t = jnp.where(group == f, both, 0.0)
-        for s in (16, 32, 64):
-            t = t + lroll(t, s)
-        spreads.append(t)
+    spreads = [jnp.where(before_half, lb[n + f], rb[n + f]) for f in range(5)]
     gst = spreads[0]
     gopw = jnp.where(group == 0, spreads[1], 0.0)
     gope = jnp.where(group == n - 1, spreads[2], 0.0)
@@ -261,21 +278,22 @@
         wide = k != 2
 
         def v(a, b):
-            return w[k - 1, a * n + b] if k else x0[a * n + b]
+            return w[k - 1, a * n + b]
 
         gv = [gw[k, b] for b in range(n)]
         gqsouth = tree([g[i] * gv[i] for i in range(n)], jnp.add)
         gqnorth = tree([g[i] * gv[n - 1 - i] for i in range(n)], jnp.add)
-        qsouth = [tree([g[i] * v(a, i) for i in range(n)], jnp.add) for a in range(n)]
-        qnorth = [tree([g[i] * v(a, n - 1 - i) for i in range(n)], jnp.add) for a in range(n)]
+        if k:
+            qsouth = [tree([g[i] * v(a, i) for i in range(n)], jnp.add) for a in range(n)]
+            qnorth = [tree([g[i] * v(a, n - 1 - i) for i in range(n)], jnp.add) for a in range(n)]
         for a in range(n):
-            below = jnp.where(lane == 0, lroll(gqnorth, -(16 * a + 5)), lroll(qnorth[a], 1))
-            above = jnp.where(lane == 127, lroll(gqsouth, 121 - 16 * a), lroll(qsouth[a], -1))
-            qf[2, a] = qsouth[a] - op[2] * below
-            qf[3, a] = qnorth[a] - op[3] * above
+            below = jnp.where(lane == 0, lroll(gqnorth, -(16 * a + 5)), lroll(qnorth[a], 1) if k else 0.0)
+            above = jnp.where(lane == 127, lroll(gqsouth, 121 - 16 * a), lroll(qsouth[a], -1) if k else 0.0)
+            qf[2, a] = qsouth[a] - op[2] * below if k else -op[2] * below
+            qf[3, a] = qnorth[a] - op[3] * above if k else -op[3] * above
         if not last:
-            mn = gather_groups(qnorth, 7)
-            ms = gather_groups(qsouth, 5)
+            mn = gather_groups(qnorth, 7) if k else mm[0]
+            ms = gather_groups(qsouth, 5) if k else mm[1]
             sterm = gqsouth - gops * jnp.where(slot16 == 6, mn, lroll(gqnorth, 1))
             nterm = gqnorth - gopn * jnp.where(slot16 == 5, ms, lroll(gqsouth, -1))
             for b in range(n):
@@ -298,6 +316,28 @@
                     gw[k + 1, b, 0:4, :] = t[0:4, :]
             if after_strip is not None:
                 after_strip()
+        if k == 0:
+            for b in range(n):
+                prev = jnp.where(sub == 4, xc[0, b], 0.0)
+                nxt = jnp.where(sub == 7, xc[1, b], 0.0)
+                prev = jnp.where(sub == 0, jnp.broadcast_to(qr[0, 1, pl.ds(b, 1), :], (8, 128)), prev)
+                nxt = jnp.where(sub == 3, jnp.broadcast_to(qr[0, 0, pl.ds(b, 1), :], (8, 128)), nxt)
+                qf[0, b] = -op[0] * prev
+                qf[1, b] = -op[1] * nxt
+            for a in range(n):
+                for b in range(n):
+                    t = w[0, a * n + b]
+                    edges = ((a == 0, 0, b), (a == n - 1, 1, b), (b == 0, 2, a), (b == n - 1, 3, a))
+                    for edge, f, i in edges:
+                        if edge:
+                            t = t + qf[f, i]
+                    if any(edge for edge, f, i in edges):
+                        w[0, a * n + b] = t
+                    if b % 2 == 0:
+                        even = t
+                    else:
+                        wp[0, (a * n + b) // 2] = pair_up(even, t)
+            return
         for b in range(n):
             qwest = tree([g[i] * v(i, b) for i in range(n)], jnp.add)
             qeast = tree([g[i] * v(n - 1 - i, b) for i in range(n)], jnp.add)
@@ -340,10 +380,7 @@
             even = None
             for b in range(n):
                 acc = tree([lop[b][i] * row[i] for i in range(n)] + [lop[a][i] * v(i, b) for i in range(n)], jnp.add)
-                if k == 0:
-                    t = rx[a * n + b] * row[b] - sv[a * n + b] + stiff * acc
-                else:
-                    t = (rx[a * n + b] - shift) * row[b] + stiff * acc
+                t = (rx[a * n + b] - shift) * row[b] + stiff * acc
                 if a == 0:
                     t = t + qf[0, b]
                 if a == n - 1:
@@ -578,15 +615,16 @@
             scratch_shapes=[
                 vm((nodes,) + tile, f32), vm((nodes,) + tile, f32), vm((nodes,) + tile, f32), vm(tile, f32),
                 vm((4,) + tile, jnp.int32), vm((4,) + tile, f32),
-                vm((NV - 1, nodes) + tile, f32), vm((nodes,) + tile, f32), vm((nodes,) + tile, f32), vm((nodes,) + tile, f32),
+                vm((NV - 1, nodes) + tile, f32), vm((nodes,) + tile, f32),
                 vm(tile, f32), vm((4,) + tile, f32), vm((NV, 8) + tile, f32),
-                vm((2, 9) + tile, f32), vm((9,) + tile, f32), vm((9,) + tile, f32),
+                vm((2, 13) + tile, f32), vm((13,) + tile, f32), vm((13,) + tile, f32),
                 vm((2, 2) + tile, f32), vm((2, 2) + tile, f32), vm((2, 2) + tile, f32), vm((1, 2) + tile, f32),
                 vm((2, 2) + tile, f32), vm((4, 8) + tile, f32),
                 vm((1, 128), f32), vm((nc * ny * nx, 1, 128), f32), vm((2, 128), f32), vm((nz, 2, 128), f32),
                 pltpu.SMEM((P_SIZE, P_SIZE), f32), pltpu.SMEM((P_SIZE,), f32),
                 vm((nodes // 2,) + tile, f32), vm((2, 16) + tile, f32),
-                dma((10,)), dma((sends,)), dma((sends,)), dma((ny * nx,)), dma((nc * ny * nx,)), dma((2 * nz - 1,)), dma((nz,)),
+                vm((2, 8) + tile, f32), vm((2,) + tile, f32),
+                dma((8,)), dma((sends,)), dma((sends,)), dma((ny * nx,)), dma((nc * ny * nx,)), dma((2 * nz - 1,)), dma((nz,)),
             ],
             compiler_params=pltpu.CompilerParams(
                 collective_id=0, has_side_effects=True, vmem_limit_bytes=48 * 1024 * 1024),

time: 32.9 us -> 32.7 us (level)
  no operation moved by 1% of the time
where the time goes in v6:
time: 32.7 us; the launch traced here: 32.6 us
  Pallas kernels  31.9 us (98%)
  between operations  0.64 us (2%)
    pallas_call x1, Pallas kernels, body(): pl.pallas_call(functools.partial(kernel, sizes), out_shape=(pltpu.VMEM((N...  30.9 us
    pallas_call x1, Pallas kernels, body(): pl.pallas_call(output_kernel, out_shape=(jax.ShapeDtypeStruct((NV, ITERS)...  1 us

profile of v6, /device:TPU:1, one launch (start us, length us, event | category | flops | bytes accessed | tf_op | source)
XLA Modules:
  0.0 32.6 jit_solution(18373657153864719917)
XLA Ops:
  0.6 30.9 %arnoldi.1 = (f32[6,32,8,128]{3,2,1,0:T(8,128)S(1)}, f32[6,8,128]{2,1,0:T(8,128)S(1)}, f32[8,128]{1,0:T(8,128)S(1)}) custom-call(f32[8,8]{1,0:T(8,128)} %line_h.1, f32[8]{0:T(128)} %fd_h.1, f32[64,4,128]{2,1,0:T(4,128)} %src_h.1, f32[64,4,128]{2,1,0:T(4,128)} %x0_h.1, f32[64,4,128]{2,1,0:T(4,128)} %rx_h.1, f32[4,128]{1,0:T(4,128)} %st_h.1, s32[4,4,128]{2,1,0:T(4,128)} %wf_h.1), custom_call_target="tpu_custom_call" | custom-call | tf_op jit(solution)/shard_map/arnoldi/pallas_call | solution.py:608
  31.6 1.0 %combine.1 = (f32[6,5]{1,0:T(8,128)}, f32[6,64,4,128]{3,2,1,0:T(4,128)}) custom-call(f32[6,32,8,128]{3,2,1,0:T(8,128)S(1)} %get-tuple-element.5.w, f32[6,8,128]{2,1,0:T(8,128)S(1)} %get-tuple-element.6.cw, f32[8,128]{1,0:T(8,128)S(1)} %get-tuple-element.7.hm), custom_call_target="tpu_custom_call" | custom-call | tf_op jit(solution)/shard_map/combine/pallas_call | solution.py:634

commit v7 on v6

--- a/solution.py
+++ b/solution.py
@@ -74,7 +74,7 @@
 
 def kernel(sizes, line_h, fd_h, src_h, x0_h, rx_h, st_h, wf_h, wp, cw, hm,
            xl, sl, rl, stl, wfl, opl, w, rx, st, op, gw, pk, lb, rb, qs, qr, gqs, gql, gqr, qf,
-           row1, buf1, row2, buf2, line, fd, rxp, cpair, xc, mm,
+           row1, buf1, row2, buf2, line, fd, rxp, cpair, xc, mm, known,
            lsem, hs, hr, s1, r1, s2, r2):
     ny, nc, nx, nz = sizes
     y, c, x, z = (lax.axis_index(a) for a in AXES)
@@ -103,21 +103,24 @@
 
     far = sorted(range(1, nz), key=lambda k: -min(k, nz - k))
     flat = sorted(range(1, ny * nx), key=lambda i: -min(i // nx, ny - i // nx) - min(i % nx, nx - i % nx))
-    for k in far:
-        greet((y, nc - 1, x, planes[k - 1]))
-    for i in flat:
-        greet((plane[i][0], nc - 1, plane[i][1], z))
-
-    @pl.when(hub)
-    def _():
-        for k in far:
-            greet((y, 0, x, planes[k - 1]))
-        for i in flat:
-            greet((plane[i][0], 0, plane[i][1], z))
-
-    for peer in around.values():
+    partner = (y, nc - 1 - c, x, z)
+    lines = {
+        "y": [(lax.rem(y + i, ny), c, x, z) for i in (1, ny - 1)],
+        "x": [(y, c, lax.rem(x + i, nx), z) for i in (1, nx - 1)],
+        "z": [(y, c, x, lax.rem(z + i, nz)) for i in (1, nz - 1)],
+    }
+    greeted = lines["y"] + lines["x"] + lines["z"] + list(around.values()) + [partner]
+    for peer in greeted:
         greet(peer)
-    greet((y, nc - 1 - c, x, z))
+
+    def tell(first, axes):
+        for i, axis in enumerate(axes):
+            for peer in lines[axis]:
+                pl.semaphore_signal(known.at[first + i], inc=1, device_id=peer, device_id_type=MESH)
+
+    def hear(first, axes):
+        for i in range(len(axes)):
+            pl.semaphore_wait(known.at[first + i], 2)
 
     for cp in loads[:2]:
         cp.wait()
@@ -175,22 +178,8 @@
         gqs[0, 1, pl.ds(b, 1), :] = qe[b][1:2, :]
         xc[0, b] = pltpu.roll(qe[b], 1, 0)
         xc[1, b] = pltpu.roll(qw[b], 7, 0)
-        qf[0, b] = qw[b] - opl[0] * jnp.where(sub == 0, 0.0, xc[0, b])
-        qf[1, b] = qe[b] - opl[1] * jnp.where(sub == 3, 0.0, xc[1, b])
-    for a in range(n):
-        qf[2, a] = qsouth[a] - opl[2] * jnp.where(lane == 0, 0.0, lroll(qnorth[a], 1))
-        qf[3, a] = qnorth[a] - opl[3] * jnp.where(lane == 127, 0.0, lroll(qsouth[a], -1))
     mm[0, 0:4, :] = gather_groups(qnorth, 7)[0:4, :]
     mm[1, 0:4, :] = gather_groups(qsouth, 5)[0:4, :]
-    for a in range(n):
-        row = [xl[a * n + i] for i in range(n)]
-        for b in range(n):
-            acc = tree([lop[b][i] * row[i] for i in range(n)] + [lop[a][i] * xl[i * n + b] for i in range(n)], jnp.add)
-            t = rl[a * n + b] * row[b] - sl[a * n + b] + stl[...] * acc
-            for edge, f, i in ((a == 0, 0, b), (a == n - 1, 1, b), (b == 0, 2, a), (b == n - 1, 3, a)):
-                if edge:
-                    t = t + qf[f, i]
-            w[0, a * n + b, 0:4, :] = t[0:4, :]
     for b in range(n):
         px = gather_groups([xl[a * n + b] for a in range(n)], 6)
         ps = gather_groups([sl[a * n + b] for a in range(n)], 6)
@@ -203,14 +192,8 @@
         spread_out = gather_groups([t] * n, 6)
         pk[0, n + f] = spread_out
         pk[1, n + f] = spread_out
-    @pl.when(hub)
-    def _():
-        pl.semaphore_wait(barrier, 8 + 31 + 14)
-
-    @pl.when(jnp.logical_not(hub))
-    def _():
-        pl.semaphore_wait(barrier, 8 + 16 + 7)
-
+    pl.semaphore_wait(barrier, len(greeted))
+    tell(0, "yz")
 
     def send(copies, peer, pieces, first):
         for i, (a, b) in enumerate(pieces):
@@ -235,18 +218,36 @@
     for dx, lo, to in ((1, 2, 6), (-1, 0, 4)):
         side = 1 if dx > 0 else 0
         used = send(copies, around[dx, 0], [
-            (w.at[0, :, rows(lo), :], w.at[0, :, rows(to), :]),
             (rl.at[:, rows(lo), :], rx.at[:, rows(to), :]),
             (mm.at[:, rows(lo), :], mm.at[:, rows(to), :]),
             (stl.at[rows(lo), :], st.at[rows(to), :]),
             (opl.at[:, rows(lo), :], op.at[:, rows(to), :]),
             (qs.at[0, side], qr.at[0, side])], used)
+    for b in range(n):
+        qf[0, b] = qw[b] - opl[0] * jnp.where(sub == 0, 0.0, xc[0, b])
+        qf[1, b] = qe[b] - opl[1] * jnp.where(sub == 3, 0.0, xc[1, b])
+    for a in range(n):
+        qf[2, a] = qsouth[a] - opl[2] * jnp.where(lane == 0, 0.0, lroll(qnorth[a], 1))
+        qf[3, a] = qnorth[a] - opl[3] * jnp.where(lane == 127, 0.0, lroll(qsouth[a], -1))
+    for a in range(n):
+        row = [xl[a * n + i] for i in range(n)]
+        for b in range(n):
+            acc = tree([lop[b][i] * row[i] for i in range(n)] + [lop[a][i] * xl[i * n + b] for i in range(n)], jnp.add)
+            t = rl[a * n + b] * row[b] - sl[a * n + b] + stl[...] * acc
+            for edge, f, i in ((a == 0, 0, b), (a == n - 1, 1, b), (b == 0, 2, a), (b == n - 1, 3, a)):
+                if edge:
+                    t = t + qf[f, i]
+            w[0, a * n + b, 0:4, :] = t[0:4, :]
+    for dx, lo, to in ((1, 2, 6), (-1, 0, 4)):
+        used = send(copies, around[dx, 0], [(w.at[0, :, rows(lo), :], w.at[0, :, rows(to), :])], used)
     st[0:4, :] = stl[0:4, :]
     op[:, 0:4, :] = opl[:, 0:4, :]
     for q in range(0, n * n, 2):
         rxp[q // 2] = jnp.where(sub < 4, rl[q], pltpu.roll(rl[q + 1], 4, 0)) - shift
     for cp in loads[7:]:
         cp.wait()
+    hear(0, "yz")
+    tell(2, "xz")
     for cp in copies:
         cp.wait()
 
@@ -397,6 +398,8 @@
 
     apply(0, fresh=0)
     apply(1)
+    hear(2, "xz")
+    tell(4, "xz")
     copies = []
     sides = ((1, 2, 6), (-1, 0, 4))
 
@@ -438,6 +441,8 @@
 
     early = [p for p in PAIRS if p[1] < 3]
     first = gram(early)
+    hear(4, "xz")
+    pl.semaphore_signal(known.at[6], inc=1, device_id=partner, device_id_type=MESH)
     for cp in copies:
         cp.wait()
     apply(3, fresh=1)
@@ -470,10 +475,9 @@
             src_ref=row2, dst_ref=buf2.at[index], send_sem=s2.at[j], recv_sem=r2.at[index],
             device_id=peer, device_id_type=MESH)
 
-    partner = (y, nc - 1 - c, x, z)
-    for j, (yy, xx) in enumerate(plane):
-        if j:
-            to_hub(j, me, (yy, nc - 1, xx, z)).start()
+    pl.semaphore_wait(known.at[6], 1)
+    for j in flat:
+        to_hub(j, me, (plane[j][0], nc - 1, plane[j][1], z)).start()
 
     @pl.when(hub)
     def _():
@@ -486,12 +490,10 @@
         total1 = tidy(total1)
         row2[0:1, :] = total1[0]
         row2[1:2, :] = total1[1]
-        k = 0
-        for zz in planes:
-            for cc in (nc - 1, 0):
-                across(k, z, (y, cc, x, zz)).start()
-                k += 1
-        across(k, z, partner).start()
+        for cc in (nc - 1, 0):
+            for k in far:
+                across(cc * len(planes) + k - 1, z, (y, cc, x, planes[k - 1])).start()
+        across(2 * len(planes), z, partner).start()
         buf2[z] = row2[...]
 
     @pl.when(jnp.logical_not(hub))
@@ -623,7 +625,7 @@
                 vm((1, 128), f32), vm((nc * ny * nx, 1, 128), f32), vm((2, 128), f32), vm((nz, 2, 128), f32),
                 pltpu.SMEM((P_SIZE, P_SIZE), f32), pltpu.SMEM((P_SIZE,), f32),
                 vm((nodes // 2,) + tile, f32), vm((2, 16) + tile, f32),
-                vm((2, 8) + tile, f32), vm((2,) + tile, f32),
+                vm((2, 8) + tile, f32), vm((2,) + tile, f32), pltpu.SemaphoreType.REGULAR((7,)),
                 dma((8,)), dma((sends,)), dma((sends,)), dma((ny * nx,)), dma((nc * ny * nx,)), dma((2 * nz - 1,)), dma((nz,)),
             ],
             compiler_params=pltpu.CompilerParams(

time: 32.7 us -> 32.1 us (0.982)
  Pallas kernels: 31.9 us -> 31.4 us
    pallas_call x1, Pallas kernels: 30.9 us -> 30.4 us  [body(): pl.pallas_call(functools.partial(kernel, sizes), out_shape=(pltpu.VMEM((N...]
where the time goes in v7:
time: 32.1 us; the launch traced here: 32 us
  Pallas kernels  31.4 us (98%)
  between operations  0.64 us (2%)
    pallas_call x1, Pallas kernels, body(): pl.pallas_call(functools.partial(kernel, sizes), out_shape=(pltpu.VMEM((N...  30.4 us
    pallas_call x1, Pallas kernels, body(): pl.pallas_call(output_kernel, out_shape=(jax.ShapeDtypeStruct((NV, ITERS)...  1 us

profile of v7, /device:TPU:1, one launch (start us, length us, event | category | flops | bytes accessed | tf_op | source)
XLA Modules:
  0.0 32.0 jit_solution(3975368849445047)
XLA Ops:
  0.6 30.4 %arnoldi.1 = (f32[6,32,8,128]{3,2,1,0:T(8,128)S(1)}, f32[6,8,128]{2,1,0:T(8,128)S(1)}, f32[8,128]{1,0:T(8,128)S(1)}) custom-call(f32[8,8]{1,0:T(8,128)} %line_h.1, f32[8]{0:T(128)} %fd_h.1, f32[64,4,128]{2,1,0:T(4,128)} %src_h.1, f32[64,4,128]{2,1,0:T(4,128)} %x0_h.1, f32[64,4,128]{2,1,0:T(4,128)} %rx_h.1, f32[4,128]{1,0:T(4,128)} %st_h.1, s32[4,4,128]{2,1,0:T(4,128)} %wf_h.1), custom_call_target="tpu_custom_call" | custom-call | tf_op jit(solution)/shard_map/arnoldi/pallas_call | solution.py:610
  31.0 1.0 %combine.1 = (f32[6,5]{1,0:T(8,128)}, f32[6,64,4,128]{3,2,1,0:T(4,128)}) custom-call(f32[6,32,8,128]{3,2,1,0:T(8,128)S(1)} %get-tuple-element.5.w, f32[6,8,128]{2,1,0:T(8,128)S(1)} %get-tuple-element.6.cw, f32[8,128]{1,0:T(8,128)S(1)} %get-tuple-element.7.hm), custom_call_target="tpu_custom_call" | custom-call | tf_op jit(solution)/shard_map/combine/pallas_call | solution.py:636

commit v8 on v7

--- a/solution.py
+++ b/solution.py
@@ -169,8 +169,6 @@
         cp.wait()
     opl[...] = 1.0 - wfl[...].astype(jnp.float32)
     qw, qe = x_faces(lambda a, b: xl[a * n + b])
-    qsouth = [tree([g[i] * xl[a * n + i] for i in range(n)], jnp.add) for a in range(n)]
-    qnorth = [tree([g[i] * xl[a * n + n - 1 - i] for i in range(n)], jnp.add) for a in range(n)]
     for b in range(n):
         qs[0, 0, pl.ds(b, 1), :] = qw[b][0:1, :]
         qs[0, 1, pl.ds(b, 1), :] = qe[b][3:4, :]
@@ -178,8 +176,6 @@
         gqs[0, 1, pl.ds(b, 1), :] = qe[b][1:2, :]
         xc[0, b] = pltpu.roll(qe[b], 1, 0)
         xc[1, b] = pltpu.roll(qw[b], 7, 0)
-    mm[0, 0:4, :] = gather_groups(qnorth, 7)[0:4, :]
-    mm[1, 0:4, :] = gather_groups(qsouth, 5)[0:4, :]
     for b in range(n):
         px = gather_groups([xl[a * n + b] for a in range(n)], 6)
         ps = gather_groups([sl[a * n + b] for a in range(n)], 6)
@@ -219,10 +215,13 @@
         side = 1 if dx > 0 else 0
         used = send(copies, around[dx, 0], [
             (rl.at[:, rows(lo), :], rx.at[:, rows(to), :]),
-            (mm.at[:, rows(lo), :], mm.at[:, rows(to), :]),
             (stl.at[rows(lo), :], st.at[rows(to), :]),
             (opl.at[:, rows(lo), :], op.at[:, rows(to), :]),
             (qs.at[0, side], qr.at[0, side])], used)
+    qsouth = [tree([g[i] * xl[a * n + i] for i in range(n)], jnp.add) for a in range(n)]
+    qnorth = [tree([g[i] * xl[a * n + n - 1 - i] for i in range(n)], jnp.add) for a in range(n)]
+    mm[0, 0:4, :] = gather_groups(qnorth, 7)[0:4, :]
+    mm[1, 0:4, :] = gather_groups(qsouth, 5)[0:4, :]
     for b in range(n):
         qf[0, b] = qw[b] - opl[0] * jnp.where(sub == 0, 0.0, xc[0, b])
         qf[1, b] = qe[b] - opl[1] * jnp.where(sub == 3, 0.0, xc[1, b])
@@ -239,7 +238,8 @@
                     t = t + qf[f, i]
             w[0, a * n + b, 0:4, :] = t[0:4, :]
     for dx, lo, to in ((1, 2, 6), (-1, 0, 4)):
-        used = send(copies, around[dx, 0], [(w.at[0, :, rows(lo), :], w.at[0, :, rows(to), :])], used)
+        used = send(copies, around[dx, 0], [
+            (w.at[0, :, rows(lo), :], w.at[0, :, rows(to), :]), (mm.at[:, rows(lo), :], mm.at[:, rows(to), :])], used)
     st[0:4, :] = stl[0:4, :]
     op[:, 0:4, :] = opl[:, 0:4, :]
     for q in range(0, n * n, 2):
@@ -450,7 +450,7 @@
     apply(5, last=True)
 
     acc = first + gram(PAIRS[len(early):])
-    line_row = jnp.zeros((8, 128), jnp.float32)
+    high = low_part = jnp.zeros((8, 128), jnp.float32)
     for base in range(0, len(PAIRS), 8):
         packed = jnp.zeros((8, 128), jnp.float32)
         for i, t in enumerate(acc[base:base + 8]):
@@ -458,12 +458,17 @@
             t = t + pltpu.roll(t, 2, 0)
             t = t + pltpu.roll(t, 1, 0)
             packed = jnp.where(sub == i, t, packed)
-        packed = jnp.sum(packed, axis=1, keepdims=True) * (1.0 / total)
-        line_row = line_row + jnp.where(lane == sub + base, packed, 0.0)
+        packed = packed * (1.0 / total)
+        bias = jnp.max(jnp.abs(packed), axis=1, keepdims=True) * 256.0
+        lead = (packed + bias) - bias
+        here = lane == sub + base
+        high = jnp.where(here, jnp.sum(lead, axis=1, keepdims=True), high)
+        low_part = jnp.where(here, jnp.sum(packed - lead, axis=1, keepdims=True), low_part)
     for s in (4, 2, 1):
-        line_row = line_row + pltpu.roll(line_row, s, 0)
-    zero1 = jnp.zeros((1, 128), jnp.float32)
-    row1[...] = line_row[0:1, :]
+        high = high + pltpu.roll(high, s, 0)
+        low_part = low_part + pltpu.roll(low_part, s, 0)
+    row1[0:1, :] = high[0:1, :]
+    row1[1:2, :] = low_part[0:1, :]
 
     def to_hub(j, index, peer):
         return pltpu.make_async_remote_copy(
@@ -486,7 +491,7 @@
             for cc in range(nc):
                 if j or cc != nc - 1:
                     to_hub(j, (cc * ny + yy) * nx + xx, partner).wait_recv()
-        total1 = tree([(buf1[j], zero1) for j in range(nc * ny * nx)], add2)
+        total1 = tree([(buf1[j, 0:1, :], buf1[j, 1:2, :]) for j in range(nc * ny * nx)], add2)
         total1 = tidy(total1)
         row2[0:1, :] = total1[0]
         row2[1:2, :] = total1[1]
@@ -622,7 +627,7 @@
                 vm((2, 13) + tile, f32), vm((13,) + tile, f32), vm((13,) + tile, f32),
                 vm((2, 2) + tile, f32), vm((2, 2) + tile, f32), vm((2, 2) + tile, f32), vm((1, 2) + tile, f32),
                 vm((2, 2) + tile, f32), vm((4, 8) + tile, f32),
-                vm((1, 128), f32), vm((nc * ny * nx, 1, 128), f32), vm((2, 128), f32), vm((nz, 2, 128), f32),
+                vm((2, 128), f32), vm((nc * ny * nx, 2, 128), f32), vm((2, 128), f32), vm((nz, 2, 128), f32),
                 pltpu.SMEM((P_SIZE, P_SIZE), f32), pltpu.SMEM((P_SIZE,), f32),
                 vm((nodes // 2,) + tile, f32), vm((2, 16) + tile, f32),
                 vm((2, 8) + tile, f32), vm((2,) + tile, f32), pltpu.SemaphoreType.REGULAR((7,)),

time: 32.1 us -> 32.5 us (1.012)
  Pallas kernels: 31.4 us -> 31.8 us
    pallas_call x1, Pallas kernels: 30.4 us -> 30.8 us  [body(): pl.pallas_call(functools.partial(kernel, sizes), out_shape=(pltpu.VMEM((N...]
where the time goes in v8:
time: 32.5 us; the launch traced here: 32.4 us
  Pallas kernels  31.8 us (98%)
  between operations  0.64 us (2%)
    pallas_call x1, Pallas kernels, body(): pl.pallas_call(functools.partial(kernel, sizes), out_shape=(pltpu.VMEM((N...  30.8 us
    pallas_call x1, Pallas kernels, body(): pl.pallas_call(output_kernel, out_shape=(jax.ShapeDtypeStruct((NV, ITERS)...  1 us

profile of v8, /device:TPU:1, one launch (start us, length us, event | category | flops | bytes accessed | tf_op | source)
XLA Modules:
  0.0 32.4 jit_solution(14413067174064687435)
XLA Ops:
  0.6 30.8 %arnoldi.1 = (f32[6,32,8,128]{3,2,1,0:T(8,128)S(1)}, f32[6,8,128]{2,1,0:T(8,128)S(1)}, f32[8,128]{1,0:T(8,128)S(1)}) custom-call(f32[8,8]{1,0:T(8,128)} %line_h.1, f32[8]{0:T(128)} %fd_h.1, f32[64,4,128]{2,1,0:T(4,128)} %src_h.1, f32[64,4,128]{2,1,0:T(4,128)} %x0_h.1, f32[64,4,128]{2,1,0:T(4,128)} %rx_h.1, f32[4,128]{1,0:T(4,128)} %st_h.1, s32[4,4,128]{2,1,0:T(4,128)} %wf_h.1), custom_call_target="tpu_custom_call" | custom-call | tf_op jit(solution)/shard_map/arnoldi/pallas_call | solution.py:615
  31.4 1.0 %combine.1 = (f32[6,5]{1,0:T(8,128)}, f32[6,64,4,128]{3,2,1,0:T(4,128)}) custom-call(f32[6,32,8,128]{3,2,1,0:T(8,128)S(1)} %get-tuple-element.5.w, f32[6,8,128]{2,1,0:T(8,128)S(1)} %get-tuple-element.6.cw, f32[8,128]{1,0:T(8,128)S(1)} %get-tuple-element.7.hm), custom_call_target="tpu_custom_call" | custom-call | tf_op jit(solution)/shard_map/combine/pallas_call | solution.py:641
